TPU v7x, 16 devices: a whole 2x2x2 slice. The times are simulated.
16 devices in a mesh: rep: 1, dp: 16 (over x, y, z, core).
Axes of the slice: x: 2, y: 2, z: 2, core: 2. Of those that a mesh axis runs over, the one named last changes fastest.
Arguments:
- x: bfloat16 [16, 2048, 1024], P(('rep', 'dp'))
- dy: bfloat16 [16, 2048, 1024], P(('rep', 'dp'))
- w_gate: bfloat16 [2, 1024, 2560], replicated
- w_up: bfloat16 [2, 1024, 2560], replicated
- w_down: bfloat16 [2, 2560, 1024], replicated
- m_w_gate: float32 [2, 1024, 2560], replicated
- m_w_up: float32 [2, 1024, 2560], replicated
- m_w_down: float32 [2, 2560, 1024], replicated
- v_w_gate: float32 [2, 1024, 2560], replicated
- v_w_up: float32 [2, 1024, 2560], replicated
- v_w_down: float32 [2, 2560, 1024], replicated
Outputs:
- output 1: bfloat16 [2, 1024, 2560], P('rep')
- output 2: bfloat16 [2, 1024, 2560], P('rep')
- output 3: bfloat16 [2, 2560, 1024], P('rep')
- output 4: float32 [2, 1024, 2560], P('rep')
- output 5: float32 [2, 1024, 2560], P('rep')
- output 6: float32 [2, 2560, 1024], P('rep')
- output 7: float32 [2, 1024, 2560], P('rep')
- output 8: float32 [2, 1024, 2560], P('rep')
- output 9: float32 [2, 2560, 1024], P('rep')
All inputs are finite; a program needn't handle non-finite values.
Results may differ from a plain program's by a relative error of at most 0.022.
Values are sent between devices in bfloat16 or wider.
A program may use at most 2.5 GiB of HBM per device.

v0:
```python
import jax
import jax.numpy as jnp
from jax import lax
from jax.sharding import PartitionSpec as P

NAMES = ("w_gate", "w_up", "w_down")


def matmul(a, w):
    return jnp.dot(a, w, preferred_element_type=jnp.float32).astype(jnp.bfloat16)


def normed(h):
    wide = h.astype(jnp.float32)
    scale = lax.rsqrt(jnp.mean(wide**2, -1, keepdims=True) + 1e-6)
    return (wide * scale).astype(jnp.bfloat16)


def layer(h, w):
    a = normed(h)
    gate = jnp.dot(a, w["w_gate"], preferred_element_type=jnp.float32)
    up = jnp.dot(a, w["w_up"], preferred_element_type=jnp.float32)
    return h + matmul((jax.nn.silu(gate) * up).astype(jnp.bfloat16), w["w_down"])


def adamw(w, m, v, g):
    m = 0.9 * m + 0.1 * g
    v = 0.95 * v + 0.05 * g * g
    step = m * lax.rsqrt(v + 1e-8) + 0.1 * w
    return (w - 0.02 * step).astype(jnp.bfloat16), m, v


def clipped(gradients, sum_of_squares, count):
    factor = jnp.minimum(1.0, 0.5 * lax.rsqrt(sum_of_squares / count + 1e-30))
    return [g * factor for g in gradients]


def solution(mesh):
    def step(x, dy, *arrays):
        weights, m, v = (arrays[i : i + 3] for i in (0, 3, 6))
        layers = weights[0].shape[0]
        h, kept = x[0], []
        for number in range(layers):
            kept.append(h)
            h = layer(h, {name: w[number] for name, w in zip(NAMES, weights, strict=True)})
        by_h, summed = dy[0], [None] * layers
        for number in reversed(range(layers)):
            _, back = jax.vjp(lambda w, h: layer(h, w), {name: w[number] for name, w in zip(NAMES, weights, strict=True)}, kept[number])
            by_w, by_h = back(by_h)
            summed[number] = [lax.psum(by_w[name], "dp") for name in NAMES]
        gradients = [jnp.stack([summed[number][i] for number in range(layers)]).astype(jnp.float32) for i in range(3)]
        gradients = clipped(gradients, sum(jnp.sum(g * g) for g in gradients), sum(g.size for g in gradients))
        new = [adamw(w.astype(jnp.float32), m, v, g) for w, m, v, g in zip(weights, m, v, gradients, strict=True)]
        return tuple(one[which] for which in range(3) for one in new)

    return jax.shard_map(
        step,
        mesh=mesh,
        in_specs=(P(("rep", "dp"), None, None),) * 2 + (P(None, None, None),) * 9,
        out_specs=(P("rep", None, None),) * 9,
        check_vma=False,
    )
```

profile of v0, /device:TPU:0, one launch (start us, length us, event | category | flops | bytes accessed | tf_op | source)
XLA Modules:
  0.0 772.3 jit_solution(12978035046329220411)
XLA Ops:
  7.2 6.5 copy.20
  16.8 6.7 copy.21
  23.5 16.9 %convolution_convert_fusion.1 = bf16[2048,2560]{1,0:T(8,128)(2,1)} fusion(bf16[2,2560,1024]{2,1,0:T(8,128)(2,1)} %param.15, bf16[1,2048,1024]{2,1,0:T(8,128)(2,1)} %param.12), kind=kOutput, calls=%fused_computation.63 | convolution fusion | flops 10742661120 | bytes 19922944 | tf_op jit(solution)/shard_map/transpose(jvp())/dot_general | solution.py:10
  40.4 14.1 %fusion.62 = f32[2048,2560]{1,0:T(8,128)} fusion(bf16[2,1024,2560]{2,1,0:T(8,128)(2,1)S(1)} %bitcast.77, bf16[1,2048,1024]{2,1,0:T(8,128)(2,1)S(1)} %copy-done.4, f32[2048]{0:T(1024)S(1)} %add_rsqrt_fusion), kind=kOutput, calls=%fused_computation.99 | convolution fusion | flops 10743709696 | bytes 30416896 | tf_op jit(solution)/shard_map/dot_general | solution.py:21
  54.5 26.7 %multiply_convert_fusion.1 = (bf16[2048,2560]{1,0:T(8,128)(2,1)}, f32[2048,2560]{1,0:T(8,128)}) fusion(f32[2048,2560]{1,0:T(8,128)} %fusion.62, bf16[2,1024,2560]{2,1,0:T(8,128)(2,1)} %param.14, bf16[1,2048,1024]{2,1,0:T(8,128)(2,1)} %param.11, f32[2048]{0:T(1024)S(1)} %add_rsqrt_fusion), kind=kOutput, calls=%fused_computation.53 | convolution fusion | flops 10775166976 | bytes 61874176 | tf_op jit(solution)/shard_map/dot_general | solution.py:22
  81.3 17.7 %fusion.40 = (f32[2048]{0:T(1024)S(1)}, bf16[2048,1024]{0,1:T(8,128)(2,1)}) fusion(bf16[2048,2560]{1,0:T(8,128)(2,1)} %get-tuple-element.24, bf16[2,2560,1024]{2,1,0:T(8,128)(2,1)} %param.15, bf16[1,2048,1024]{1,2,0:T(8,128)(2,1)S(1)} %copy-done.2), kind=kOutput, calls=%fused_computation.76 | convolution fusion | flops 10747901952 | bytes 24125440 | tf_op jit(solution)/shard_map/dot_general | solution.py:10
  98.9 18.5 %fusion.49 = f32[2048,2560]{1,0:T(8,128)} fusion(bf16[2,1024,2560]{2,1,0:T(8,128)(2,1)} %param.14, bf16[2048,1024]{0,1:T(8,128)(2,1)} %get-tuple-element.27, f32[2048]{0:T(1024)S(1)} %fusion.98), kind=kOutput, calls=%fused_computation.86 | convolution fusion | flops 10743709696 | bytes 30416896 | tf_op jit(solution)/shard_map/jvp()/dot_general | solution.py:22
  117.4 32.5 %fusion.20 = (bf16[2048,2560]{1,0:T(8,128)(2,1)}, f32[2048,2560]{1,0:T(8,128)}) fusion(f32[2048,2560]{1,0:T(8,128)} %fusion.49, bf16[2048,2560]{1,0:T(8,128)(2,1)} %convolution_convert_fusion.1, bf16[2,1024,2560]{2,1,0:T(8,128)(2,1)} %param.13, bf16[2048,1024]{0,1:T(8,128)(2,1)} %get-tuple-element.27, f32[2048]{0:T(1024)S(1)} %fusion.98), kind=kOutput, calls=%fused_computation.41 | convolution fusion | flops 10806624256 | bytes 72359936 | tf_op jit(solution)/shard_map/jvp()/dot_general | solution.py:21
  149.9 19.9 %fusion.33 = bf16[2048,1024]{0,1:T(8,128)(2,1)} fusion(bf16[2048,2560]{1,0:T(8,128)(2,1)} %convolution_convert_fusion.1, bf16[2,1024,2560]{2,1,0:T(8,128)(2,1)} %param.14, f32[2048,2560]{1,0:T(8,128)} %get-tuple-element.29), kind=kOutput, calls=%fused_computation.61 | convolution fusion | flops 10768875520 | bytes 40894464 | tf_op jit(solution)/shard_map/transpose(jvp())/dot_general | solution.py:22
  169.8 20.0 %fusion.71 = bf16[1,1024,2560]{2,1,0:T(8,128)(2,1)} fusion(bf16[2048,2560]{1,0:T(8,128)(2,1)} %convolution_convert_fusion.1, bf16[2048,1024]{0,1:T(8,128)(2,1)} %get-tuple-element.27, f32[2048]{0:T(1024)S(1)} %fusion.98, f32[2048,2560]{1,0:T(8,128)} %get-tuple-element.29), kind=kOutput, calls=%fused_computation.106 | convolution fusion | flops 10777788416 | bytes 40902656 | tf_op jit(solution)/shard_map/transpose(jvp())/dot_general | solution.py:22
  189.8 22.1 %fusion.72 = bf16[1,2560,1024]{2,1,0:T(8,128)(2,1)} fusion(f32[2048,2560]{1,0:T(8,128)} %fusion.49, bf16[1,2048,1024]{2,1,0:T(8,128)(2,1)} %param.12, f32[2048,2560]{1,0:T(8,128)} %get-tuple-element.29), kind=kOutput, calls=%fused_computation.107 | convolution fusion | flops 10771496960 | bytes 51380224 | tf_op jit(solution)/shard_map/transpose(jvp())/dot_general | solution.py:10
  211.9 16.6 %fusion.73 = bf16[1,1024,2560]{2,1,0:T(8,128)(2,1)} fusion(bf16[2048,2560]{1,0:T(8,128)(2,1)} %get-tuple-element.28, bf16[2048,1024]{0,1:T(8,128)(2,1)} %get-tuple-element.27, f32[2048]{0:T(1024)S(1)} %fusion.98), kind=kOutput, calls=%fused_computation.108 | convolution fusion | flops 10743709696 | bytes 19931136 | tf_op jit(solution)/shard_map/transpose(jvp())/dot_general | solution.py:21
  228.5 16.8 %fusion.42 = (f32[2048]{0:T(1024)S(1)}, bf16[2048,1024]{0,1:T(8,128)(2,1)S(1)}) fusion(bf16[2048,1024]{0,1:T(8,128)(2,1)S(1)} %copy-done.3, bf16[2048,1024]{0,1:T(8,128)(2,1)} %fusion.33, bf16[2048,2560]{1,0:T(8,128)(2,1)} %get-tuple-element.28, bf16[2,1024,2560]{2,1,0:T(8,128)(2,1)} %param.13), kind=kOutput, calls=%fused_computation.78 | convolution fusion | flops 10747901952 | bytes 28319744 | tf_op jit(solution)/shard_map/transpose(jvp())/dot_general | solution.py:21
  245.4 3.2 fusion.82
  248.5 15.8 %convolution_convert_fusion = bf16[2048,2560]{1,0:T(8,128)(2,1)} fusion(bf16[2048,1024]{0,1:T(8,128)(2,1)S(1)} %fusion.82, bf16[2,2560,1024]{2,1,0:T(8,128)(2,1)} %param.15), kind=kOutput, calls=%fused_computation.62 | convolution fusion | flops 10742661120 | bytes 19922944 | tf_op jit(solution)/shard_map/transpose(jvp())/dot_general | solution.py:10
  264.4 15.6 %fusion.74 = bf16[1,2560,1024]{2,1,0:T(8,128)(2,1)} fusion(bf16[2048,2560]{1,0:T(8,128)(2,1)} %get-tuple-element.24, bf16[2048,1024]{0,1:T(8,128)(2,1)S(1)} %fusion.82), kind=kOutput, calls=%fused_computation.109 | convolution fusion | flops 10740039680 | bytes 19922944 | tf_op jit(solution)/shard_map/transpose(jvp())/dot_general | solution.py:10
  280.0 20.0 %fusion.67 = bf16[1,1024,2560]{2,1,0:T(8,128)(2,1)} fusion(bf16[2048,2560]{1,0:T(8,128)(2,1)} %convolution_convert_fusion, bf16[1,2048,1024]{1,2,0:T(8,128)(2,1)} %copy.20, f32[2048]{0:T(1024)S(1)} %copy-done.8, f32[2048,2560]{1,0:T(8,128)} %fusion.62), kind=kOutput, calls=%fused_computation.104 | convolution fusion | flops 10777788416 | bytes 40902656 | tf_op jit(solution)/shard_map/transpose(jvp())/dot_general | solution.py:22
  299.9 25.0 %fusion.68 = bf16[1,1024,2560]{2,1,0:T(8,128)(2,1)} fusion(f32[2048,2560]{1,0:T(8,128)} %fusion.62, f32[2048,2560]{1,0:T(8,128)} %get-tuple-element.25, bf16[2048,2560]{1,0:T(8,128)(2,1)} %convolution_convert_fusion, bf16[1,2048,1024]{1,2,0:T(8,128)(2,1)} %copy.20, f32[2048]{0:T(1024)S(1)} %copy-done.8), kind=kOutput, calls=%fused_computation.105 | convolution fusion | flops 10804002816 | bytes 61874176 | tf_op jit(solution)/shard_map/transpose(jvp())/dot_general | solution.py:21
  324.9 301.2 %all-reduce.3.cloned.1.call-done = (bf16[1,1024,2560]{2,1,0:T(8,128)(2,1)}, bf16[1,1024,2560]{2,1,0:T(8,128)(2,1)}, bf16[1,1024,2560]{2,1,0:T(8,128)(2,1)}, bf16...) async-done(((bf16[1,1024,2560]{2,1,0:T(8,128)(2,1)}, bf16[1,1024,2560]{2,1,0:T(8,128)(2,1)}, ...) | async-done | bytes 31457296 | tf_op jit(solution)/shard_map/psum | solution.py:50
  626.1 9.4 %fusion.10 = f32[]{:T(128)} fusion(bf16[1,1024,2560]{2,1,0:T(8,128)(2,1)} %get-tuple-element.9, bf16[1,1024,2560]{2,1,0:T(8,128)(2,1)} %get-tuple-element.10), kind=kLoop, calls=%fused_computation.31 | loop fusion | flops 20971520 | bytes 10485764 | tf_op jit(solution)/shard_map/reduce_sum | solution.py:52
  635.6 6.0 fusion.11
  642.9 8.5 %fusion.12 = f32[]{:T(128)} fusion(bf16[1,2560,1024]{2,1,0:T(8,128)(2,1)} %get-tuple-element.13, bf16[1,2560,1024]{2,1,0:T(8,128)(2,1)} %get-tuple-element.14), kind=kLoop, calls=%fused_computation.33 | loop fusion | flops 20971520 | bytes 10485764 | tf_op jit(solution)/shard_map/reduce_sum | solution.py:52
  652.1 40.1 %fusion.18 = (bf16[2,2560,1024]{2,1,0:T(8,128)(2,1)}, f32[2,2560,1024]{2,1,0:T(8,128)}, f32[2,2560,1024]{2,1,0:T(8,128)}) fusion(bf16[2,2560,1024]{2,1,0:T(8,128)(2,1)} %param.15, f32[]{:T(128)S(6)} %min_shard_map.3, bf16[1,2560,1024]{2,1,0:T(8,128)(2,1)} %get-tuple-element.13, bf16[1,2560,1024]{2,1,0:T(8,128)(2,1)} %get-tuple-element.14, ...), kind=kLoop, calls=%fused_computation.39 | loop fusion | flops 104857600 | bytes 115343360 | tf_op jit(solution)/shard_map/convert_element_type | solution.py:30
  692.2 72.8 %fusion.8 = (bf16[2,1024,2560]{2,1,0:T(8,128)(2,1)}, f32[2,1024,2560]{2,1,0:T(8,128)}, f32[2,1024,2560]{2,1,0:T(8,128)}, bf16[2,1024,2560]{2,1,0:T(8,128)(2,1)},...) fusion(bf16[2,1024,2560]{2,1,0:T(8,128)(2,1)} %param.13, f32[]{:T(128)S(6)} %min_shard_map.3, ...), kind=kLoop, calls=%fused_computation.29 | loop fusion | flops 209715200 | bytes 230686720 | tf_op jit(solution)/shard_map/convert_element_type | solution.py:30
  (36 shorter events, 3.2 us)
Async XLA Ops:
  7.2 618.9 %all-reduce.3.cloned.1.call-start = ((), (), s32[]{:S(2)}) async-start(), calls=%async_computation | async-start | bytes 62914560 | tf_op jit(solution)/shard_map/psum | solution.py:50
  16.8 37.7 %copy-start.7 = (f32[2048]{0:T(1024)}, f32[2048]{0:T(1024)S(1)}, u32[]{:S(2)}) copy-start(f32[2048]{0:T(1024)S(1)} %add_rsqrt_fusion) | copy-start | bytes 24580
  16.8 23.6 %slice-start.2 = ((s8[10485760]{0:T(1024)(128)(4,1)}), s8[2097152]{0:T(1024)(128)(4,1)S(1)}, s32[]{:S(2)}) async-start(s8[10485760]{0:T(1024)(128)(4,1)} %bitcast.76), calls=%async_computation.3 | async-start | bytes 4194304
  23.5 16.9 %slice-start.3 = ((s8[10485760]{0:T(1024)(128)(4,1)}), s8[4194304]{0:T(1024)(128)(4,1)S(1)}, s32[]{:S(2)}) async-start(s8[10485760]{0:T(1024)(128)(4,1)} %bitcast.76), calls=%async_computation.4 | async-start | bytes 8388608
  23.5 16.9 %slice-start.4 = ((s8[10485760]{0:T(1024)(128)(4,1)}), s8[4194304]{0:T(1024)(128)(4,1)S(1)}, s32[]{:S(2)}) async-start(s8[10485760]{0:T(1024)(128)(4,1)} %bitcast.76), calls=%async_computation.5 | async-start | bytes 8388608
  23.5 16.9 %copy-start.4 = (bf16[1,2048,1024]{2,1,0:T(8,128)(2,1)S(1)}, bf16[1,2048,1024]{2,1,0:T(8,128)(2,1)}, u32[]{:S(2)}) copy-start(bf16[1,2048,1024]{2,1,0:T(8,128)(2,1)} %param.11) | copy-start | bytes 12582916
  54.5 26.7 %copy-start.2 = (bf16[1,2048,1024]{1,2,0:T(8,128)(2,1)S(1)}, bf16[1,2048,1024]{1,2,0:T(8,128)(2,1)}, u32[]{:S(2)}) copy-start(bf16[1,2048,1024]{1,2,0:T(8,128)(2,1)} %copy.20) | copy-start | bytes 12582916
  98.9 18.5 %copy-start.5 = (f32[2048]{0:T(1024)}, f32[2048]{0:T(1024)S(1)}, u32[]{:S(2)}) copy-start(f32[2048]{0:T(1024)S(1)} %get-tuple-element.26) | copy-start | bytes 24580
  211.9 16.6 %copy-start.3 = (bf16[2048,1024]{0,1:T(8,128)(2,1)S(1)}, bf16[2048,1024]{0,1:T(8,128)(2,1)}, u32[]{:S(2)}) copy-start(bf16[2048,1024]{0,1:T(8,128)(2,1)} %get-tuple-element.27) | copy-start | bytes 12582916
  228.5 16.8 %copy-start.6 = (f32[2048]{0:T(1024)S(1)}, f32[2048]{0:T(1024)}, u32[]{:S(2)}) copy-start(f32[2048]{0:T(1024)} %copy-done.5) | copy-start | bytes 24580
  228.5 16.9 %copy-start.1 = (bf16[1,2048,1024]{1,2,0:T(8,128)(2,1)S(1)}, bf16[1,2048,1024]{1,2,0:T(8,128)(2,1)}, u32[]{:S(2)}) copy-start(bf16[1,2048,1024]{1,2,0:T(8,128)(2,1)} %copy.21) | copy-start | bytes 12582916
  264.4 15.6 %copy-start.8 = (f32[2048]{0:T(1024)S(1)}, f32[2048]{0:T(1024)}, u32[]{:S(2)}) copy-start(f32[2048]{0:T(1024)} %copy-done.7) | copy-start | bytes 24580
  626.1 9.5 %slice-start = ((s8[5242880]{0:T(1024)(128)(4,1)}), s8[4194304]{0:T(1024)(128)(4,1)S(1)}, s32[]{:S(2)}) async-start(s8[5242880]{0:T(1024)(128)(4,1)} %bitcast.74), calls=%async_computation.1 | async-start | bytes 8388608
  626.1 9.5 %copy-start = (bf16[1,1024,2560]{2,1,0:T(8,128)(2,1)S(1)}, bf16[1,1024,2560]{2,1,0:T(8,128)(2,1)}, u32[]{:S(2)}) copy-start(bf16[1,1024,2560]{2,1,0:T(8,128)(2,1)} %get-tuple-element.12) | copy-start | bytes 15728644
  626.1 9.5 %slice-start.1 = ((s8[5242880]{0:T(1024)(128)(4,1)}), s8[1048576]{0:T(1024)(128)(4,1)S(1)}, s32[]{:S(2)}) async-start(s8[5242880]{0:T(1024)(128)(4,1)} %bitcast.74), calls=%async_computation.2 | async-start | bytes 2097152
Sparse Core Ops, SparseCore 0:
  325.0 301.0 all-reduce.2
where the time goes:
time: 781 us; the launch traced here: 772 us
  waiting for transfers between devices  301 us (39%)
  matrix products  298 us (38%)
  other arithmetic  143 us (18%)
  between operations  16.6 us (2%)
  local copies, waits for them, and re-layouts  13.2 us (2%)
    psum x1, waiting for transfers between devices, step(): summed[number] = [lax.psum(by_w[name], 'dp') for name in NAMES]  301 us
    convert_element_type x2, other arithmetic, adamw(): return ((w - 0.02 * step).astype(jnp.bfloat16), m, v)  113 us
    dot_general x5, matrix products, layer(): up = jnp.dot(a, w['w_up'], preferred_element_type=jnp.float32)  105 us
    dot_general x5, matrix products, layer(): gate = jnp.dot(a, w['w_gate'], preferred_element_type=jnp.float32)  105 us
    dot_general x5, matrix products, matmul(): jnp.dot(a, w, preferred_element_type=jnp.float32).astype(jnp.bfloat16)  88.1 us
    reduce_sum x3, other arithmetic, step(): jnp.sum(g * g)  24 us
  transfers between devices with their start and end apart: 1, of which 1 were waited for; matrix products, arithmetic and copies ran while one was open for 0% of the time, Pallas kernels for 0%

commit v1 on v0

v1 whole, which is shorter than its diff:
```python
import functools
import jax
import jax.numpy as jnp
from jax import lax
from jax.experimental import pallas as pl
from jax.experimental.pallas import tpu as pltpu
from jax.sharding import PartitionSpec as P

T, D, F = 2048, 1024, 2560
FT = 512
NT = F // FT
MB = 512
BF, F32 = jnp.bfloat16, jnp.float32
VL = 64 * 1024 * 1024 - 128 * 1024
NN = (((1,), (0,)), ((), ()))
NTR = (((1,), (1,)), ((), ()))


def dot(a, b, dims=NN):
    return lax.dot_general(a, b, dims, preferred_element_type=F32)


def params():
    return pltpu.CompilerParams(vmem_limit_bytes=VL, dimension_semantics=("arbitrary",))


def norm_block(h):
    wide = h.astype(F32)
    scale = lax.rsqrt(jnp.mean(wide * wide, -1, keepdims=True) + 1e-6)
    return (wide * scale).astype(BF)


def rows(i, n):
    return pl.ds(pl.multiple_of(i * n, n), n)


def norm_into(h_ref, a_ref, at_ref, n=256):
    def body(i, _):
        a = norm_block(h_ref[rows(i, n), :])
        if a_ref is not None:
            a_ref[rows(i, n), :] = a
        if at_ref is not None:
            at_ref[:, rows(i, n)] = a.T
        return 0
    lax.fori_loop(0, T // n, body, 0)


def transpose_into(h_ref, at_ref, n=256):
    def body(i, _):
        at_ref[:, rows(i, n)] = h_ref[rows(i, n), :].T
        return 0
    lax.fori_loop(0, T // n, body, 0)


def kernel_a(x_ref, wg_ref, wu_ref, wd_ref, gate_ref, up_ref, h1_ref, a_ref, acc_ref):
    t = pl.program_id(0)

    @pl.when(t == 0)
    def _():
        norm_into(x_ref, a_ref, None)

    def body(first, i, _):
        r = rows(i, MB)
        a = a_ref[r, :]
        gate = dot(a, wg_ref[0])
        up = dot(a, wu_ref[0])
        gate_ref[r, :] = gate
        up_ref[r, :] = up
        hid = (gate * jax.nn.sigmoid(gate) * up).astype(BF)
        y = dot(hid, wd_ref[0])
        if first:
            acc_ref[r, :] = y
        else:
            acc_ref[r, :] += y
        return 0

    @pl.when(t == 0)
    def _():
        lax.fori_loop(0, T // MB, functools.partial(body, True), 0)

    @pl.when(t > 0)
    def _():
        lax.fori_loop(0, T // MB, functools.partial(body, False), 0)

    @pl.when(t == NT - 1)
    def _():
        def fin(i, _):
            r = rows(i, MB)
            h1_ref[r, :] = (x_ref[r, :].astype(F32) + acc_ref[r, :].astype(BF).astype(F32)).astype(BF)
            return 0
        lax.fori_loop(0, T // MB, fin, 0)


def forward0(x, wg, wu, wd):
    whole = pl.BlockSpec((T, D), lambda t: (0, 0), pipeline_mode=pl.Buffered(1))
    return pl.pallas_call(
        kernel_a,
        grid=(NT,),
        in_specs=[whole,
                  pl.BlockSpec((1, D, FT), lambda t: (0, 0, t)),
                  pl.BlockSpec((1, D, FT), lambda t: (0, 0, t)),
                  pl.BlockSpec((1, FT, D), lambda t: (0, t, 0))],
        out_specs=[pl.BlockSpec((T, FT), lambda t: (0, t)), pl.BlockSpec((T, FT), lambda t: (0, t)), pl.BlockSpec((T, D), lambda t: (0, 0))],
        out_shape=[jax.ShapeDtypeStruct((T, F), F32), jax.ShapeDtypeStruct((T, F), F32), jax.ShapeDtypeStruct((T, D), BF)],
        scratch_shapes=[pltpu.VMEM((T, D), BF), pltpu.VMEM((T, D), F32)],
        compiler_params=params(),
        cost_estimate=pl.CostEstimate(flops=6 * T * D * F, bytes_accessed=8 * T * F + 6 * D * F, transcendentals=0),
        name="fwd0",
    )(x, wg, wu, wd)


def back_elementwise(gate, up, dhid):
    s = jax.nn.sigmoid(gate)
    silu = gate * s
    dh = dhid.astype(BF).astype(F32)
    hid = (silu * up).astype(BF)
    du = (dh * silu).astype(BF)
    dg = (dh * up * (s + silu * (1.0 - s))).astype(BF)
    return hid, dg, du


def weight_grads(at_ref, dt_ref, hid_ref, dg_ref, du_ref, g_ref):
    def body(n, _):
        r = rows(n, 256)
        at = at_ref[r, :]
        g_ref[0, r, :] = dot(at, dg_ref[...]).astype(BF)
        g_ref[1, r, :] = dot(at, du_ref[...]).astype(BF)
        g_ref[2, r, :] = dot(dt_ref[r, :], hid_ref[...]).astype(BF)
        return 0
    lax.fori_loop(0, D // 256, body, 0)


def kernel_b(h_ref, dy_ref, wg_ref, wu_ref, wd_ref, g_ref, dh_ref, a_ref, at_ref, dt_ref, accg_ref, accu_ref, hid_ref, dg_ref, du_ref):
    t = pl.program_id(0)

    @pl.when(t == 0)
    def _():
        norm_into(h_ref, a_ref, at_ref)
        transpose_into(dy_ref, dt_ref)

    def body(first, i, _):
        r = rows(i, MB)
        a = a_ref[r, :]
        gate = dot(a, wg_ref[0])
        up = dot(a, wu_ref[0])
        dhid = dot(dy_ref[r, :], wd_ref[0], NTR)
        hid, dg, du = back_elementwise(gate, up, dhid)
        hid_ref[r, :] = hid
        dg_ref[r, :] = dg
        du_ref[r, :] = du
        yg = dot(dg, wg_ref[0], NTR)
        yu = dot(du, wu_ref[0], NTR)
        if first:
            accg_ref[r, :] = yg
            accu_ref[r, :] = yu
        else:
            accg_ref[r, :] += yg
            accu_ref[r, :] += yu
        return 0

    @pl.when(t == 0)
    def _():
        lax.fori_loop(0, T // MB, functools.partial(body, True), 0)

    @pl.when(t > 0)
    def _():
        lax.fori_loop(0, T // MB, functools.partial(body, False), 0)

    weight_grads(at_ref, dt_ref, hid_ref, dg_ref, du_ref, g_ref)

    @pl.when(t == NT - 1)
    def _():
        def fin(i, _):
            r = rows(i, 256)
            wide = h_ref[r, :].astype(F32)
            scale = lax.rsqrt(jnp.mean(wide * wide, -1, keepdims=True) + 1e-6)
            da = (accg_ref[r, :].astype(BF).astype(F32) + accu_ref[r, :].astype(BF).astype(F32)).astype(BF).astype(F32)
            inner = jnp.mean(da * wide, -1, keepdims=True)
            dn = (da * scale - wide * (scale * scale * scale * inner)).astype(BF).astype(F32)
            dh_ref[r, :] = (dy_ref[r, :].astype(F32) + dn).astype(BF)
            return 0
        lax.fori_loop(0, T // 256, fin, 0)


def layer1(h1, dy, wg, wu, wd):
    whole = pl.BlockSpec((T, D), lambda t: (0, 0), pipeline_mode=pl.Buffered(1))
    return pl.pallas_call(
        kernel_b,
        grid=(NT,),
        in_specs=[whole, whole,
                  pl.BlockSpec((1, D, FT), lambda t: (1, 0, t)),
                  pl.BlockSpec((1, D, FT), lambda t: (1, 0, t)),
                  pl.BlockSpec((1, FT, D), lambda t: (1, t, 0))],
        out_specs=[pl.BlockSpec((3, D, FT), lambda t: (0, 0, t)), pl.BlockSpec((T, D), lambda t: (0, 0), pipeline_mode=pl.Buffered(1))],
        out_shape=[jax.ShapeDtypeStruct((3, D, F), BF), jax.ShapeDtypeStruct((T, D), BF)],
        scratch_shapes=[pltpu.VMEM((T, D), BF), pltpu.VMEM((D, T), BF), pltpu.VMEM((D, T), BF), pltpu.VMEM((T, D), F32), pltpu.VMEM((T, D), F32),
                        pltpu.VMEM((T, FT), BF), pltpu.VMEM((T, FT), BF), pltpu.VMEM((T, FT), BF)],
        compiler_params=params(),
        cost_estimate=pl.CostEstimate(flops=16 * T * D * F, bytes_accessed=12 * D * F + 6 * T * D, transcendentals=0),
        name="layer1",
    )(h1, dy, wg, wu, wd)


def kernel_c(x_ref, dh_ref, gate_ref, up_ref, wd_ref, g_ref, at_ref, dt_ref, hid_ref, dg_ref, du_ref):
    t = pl.program_id(0)

    @pl.when(t == 0)
    def _():
        norm_into(x_ref, None, at_ref)
        transpose_into(dh_ref, dt_ref)

    def body(i, _):
        r = rows(i, MB)
        dhid = dot(dh_ref[r, :], wd_ref[0], NTR)
        hid, dg, du = back_elementwise(gate_ref[r, :], up_ref[r, :], dhid)
        hid_ref[r, :] = hid
        dg_ref[r, :] = dg
        du_ref[r, :] = du
        return 0
    lax.fori_loop(0, T // MB, body, 0)
    weight_grads(at_ref, dt_ref, hid_ref, dg_ref, du_ref, g_ref)


def back0(x, dh1, gate, up, wd):
    whole = pl.BlockSpec((T, D), lambda t: (0, 0), pipeline_mode=pl.Buffered(1))
    return pl.pallas_call(
        kernel_c,
        grid=(NT,),
        in_specs=[whole, whole, pl.BlockSpec((T, FT), lambda t: (0, t)), pl.BlockSpec((T, FT), lambda t: (0, t)),
                  pl.BlockSpec((1, FT, D), lambda t: (0, t, 0))],
        out_specs=pl.BlockSpec((3, D, FT), lambda t: (0, 0, t)),
        out_shape=jax.ShapeDtypeStruct((3, D, F), BF),
        scratch_shapes=[pltpu.VMEM((D, T), BF), pltpu.VMEM((D, T), BF),
                        pltpu.VMEM((T, FT), BF), pltpu.VMEM((T, FT), BF), pltpu.VMEM((T, FT), BF)],
        compiler_params=params(),
        cost_estimate=pl.CostEstimate(flops=8 * T * D * F, bytes_accessed=8 * T * F + 8 * D * F, transcendentals=0),
        name="back0",
    )(x, dh1, gate, up, wd)


def adamw_into(w_ref, m_ref, v_ref, g, wo_ref, mo_ref, vo_ref):
    m = 0.9 * m_ref[0] + 0.1 * g
    v = 0.95 * v_ref[0] + 0.05 * g * g
    w = w_ref[0].astype(F32)
    wo_ref[0] = (w - 0.02 * (m * lax.rsqrt(v + 1e-8) + 0.1 * w)).astype(BF)
    mo_ref[0] = m
    vo_ref[0] = v


def kernel_o(f_ref, g_ref, *refs):
    ins, outs = refs[:9], refs[-9:]
    factor = f_ref[0, 0]
    for i in range(3):
        g = g_ref[i].astype(F32)
        if i == 2:
            g = g.T
        adamw_into(ins[i], ins[3 + i], ins[6 + i], g * factor, outs[i], outs[3 + i], outs[6 + i])


def optimizer(layer, factor, g, arrays, before):
    fb = 256
    wide = pl.BlockSpec((1, D, fb), lambda t: (layer, 0, t))
    tall = pl.BlockSpec((1, fb, D), lambda t: (layer, t, 0))
    three = [wide, wide, tall]
    alias = {} if before is None else {11 + i: i for i in range(9)}
    return pl.pallas_call(
        kernel_o,
        grid=(F // fb,),
        in_specs=[pl.BlockSpec(memory_space=pltpu.SMEM), pl.BlockSpec((3, D, fb), lambda t: (0, 0, t))] + three * 3
        + ([] if before is None else [pl.BlockSpec(memory_space=pl.ANY)] * 9),
        out_specs=three * 3,
        out_shape=[jax.ShapeDtypeStruct(a.shape, a.dtype) for a in arrays],
        input_output_aliases=alias,
        compiler_params=params(),
        cost_estimate=pl.CostEstimate(flops=30 * D * F, bytes_accessed=66 * D * F, transcendentals=3 * D * F),
        name=f"adamw{layer}",
    )(factor, g, *arrays, *(before or ()))


def solution(mesh):
    def step(x, dy, *arrays):
        wg, wu, wd = arrays[:3]
        gate, up, h1 = forward0(x[0], wg, wu, wd)
        g1, dh1 = layer1(h1, dy[0], wg, wu, wd)
        s1 = lax.psum_scatter(g1.reshape(3 * D, F), "dp", scatter_dimension=0, tiled=True)
        g0 = back0(x[0], dh1, gate, up, wd)
        g0, s1 = lax.optimization_barrier((g0, s1))
        s0 = lax.psum_scatter(g0.reshape(3 * D, F), "dp", scatter_dimension=0, tiled=True)
        squares = lax.psum(sum(jnp.sum(s.astype(F32) ** 2) for s in (s0, s1)), "dp")
        factor = jnp.minimum(1.0, 0.5 * lax.rsqrt(squares / (6 * D * F) + 1e-30)).reshape(1, 1)
        a1 = lax.all_gather(s1, "dp", axis=0, tiled=True)
        a0 = lax.all_gather(s0, "dp", axis=0, tiled=True)
        out = optimizer(1, factor, a1.reshape(3, D, F), arrays, None)
        return tuple(optimizer(0, factor, a0.reshape(3, D, F), arrays, out))

    return jax.shard_map(
        step,
        mesh=mesh,
        in_specs=(P(("rep", "dp"), None, None),) * 2 + (P(None, None, None),) * 9,
        out_specs=(P("rep", None, None),) * 9,
        check_vma=False,
    )
```

time: 781 us -> 601 us (0.77); the launches traced: 772 us -> 601 us
  Pallas kernels: 0 us -> 347 us
  matrix products: 298 us -> 0 us
  other arithmetic: 143 us -> 3.42 us
  waiting for transfers between devices: 301 us -> 202 us
  blocking collectives: 0 us -> 32.3 us
  local copies, waits for them, and re-layouts: 13.2 us -> 0.01 us
    pallas_call x0 -> x5, Pallas kernels: none -> 347 us  [the longest x1 116 us: layer1(): pl.pallas_call(kernel_b, grid=(NT,), in_specs=[whole, whole, pl.BlockSpec...]
    psum x1 -> x0, waiting for transfers between devices: 301 us -> none  [step(): summed[number] = [lax.psum(by_w[name], 'dp') for name in NAMES]]
    dot_general x15 -> x0, matrix products: 298 us -> none  [the longest x5 105 us: layer(): up = jnp.dot(a, w['w_up'], preferred_element_type=jnp.float32)]
    reduce_scatter x0 -> x2, waiting for transfers between devices: none -> 145 us  [the longest x1 108 us: step(): lax.psum_scatter(g0.reshape(3 * D, F), 'dp', scatter_dimension=0, tiled=T...]
    convert_element_type x2 -> x0, other arithmetic: 113 us -> none  [adamw(): return ((w - 0.02 * step).astype(jnp.bfloat16), m, v)]
    all_gather x0 -> x2, waiting for transfers between devices: none -> 55.9 us  [the longest x1 38.1 us: step(): a1 = lax.all_gather(s1, 'dp', axis=0, tiled=True)]
    psum x0 -> x1, blocking collectives: none -> 32.3 us  [step(): lax.psum(sum((jnp.sum(s.astype(F32) ** 2) for s in (s0, s1))), 'dp')]
    reduce_sum x4 -> x2, other arithmetic: 27 us -> 3.42 us  [step(): jnp.sum(s.astype(F32) ** 2)]
  transfers between devices with their start and end apart: 1 -> 4, of which waited for: 1 -> 4; matrix products, arithmetic and copies ran while one was open for 0% -> 1% of each run, Pallas kernels for 0% -> 21%
where the time goes in v1:
time: 601 us
  Pallas kernels  347 us (58%)
  waiting for transfers between devices  202 us (34%)
  blocking collectives  32.3 us (5%)
  between operations  15.8 us (3%)
    pallas_call x1, Pallas kernels, layer1(): pl.pallas_call(kernel_b, grid=(NT,), in_specs=[whole, whole, pl.BlockSpec...  116 us
    pallas_call x2, Pallas kernels, optimizer(): pl.pallas_call(kernel_o, grid=(F // fb,), in_specs=[pl.BlockSpec(memory_s...  114 us
    reduce_scatter x1, waiting for transfers between devices, step(): lax.psum_scatter(g0.reshape(3 * D, F), 'dp', scatter_dimension=0, tiled=T...  108 us
    pallas_call x1, Pallas kernels, back0(): pl.pallas_call(kernel_c, grid=(NT,), in_specs=[whole, whole, pl.BlockSpec...  70.1 us
    pallas_call x1, Pallas kernels, forward0(): pl.pallas_call(kernel_a, grid=(NT,), in_specs=[whole, pl.BlockSpec((1, D,...  47.2 us
    all_gather x1, waiting for transfers between devices, step(): a1 = lax.all_gather(s1, 'dp', axis=0, tiled=True)  38.1 us
    reduce_scatter x1, waiting for transfers between devices, step(): lax.psum_scatter(g1.reshape(3 * D, F), 'dp', scatter_dimension=0, tiled=T...  36.6 us
    psum x1, blocking collectives, step(): lax.psum(sum((jnp.sum(s.astype(F32) ** 2) for s in (s0, s1))), 'dp')  32.3 us
  transfers between devices with their start and end apart: 4, of which 4 were waited for; matrix products, arithmetic and copies ran while one was open for 1% of the time, Pallas kernels for 21%

profile of v1, /device:TPU:0, one launch (start us, length us, event | category | flops | bytes accessed | tf_op | source)
XLA Modules:
  0.0 600.6 jit_solution(1689173960364366007)
XLA Ops:
  7.2 0.0 reduce-scatter.3.cloned.1.call-start
  7.2 47.2 %fwd0.1 = (f32[2048,2560]{1,0:T(8,128)}, f32[2048,2560]{1,0:T(8,128)}, bf16[2048,1024]{1,0:T(8,128)(2,1)}) custom-call(bf16[2048,1024]{1,0:T(8,128)(2,1)} %bitcast.12, bf16[2,1024,2560]{2,1,0:T(8,128)(2,1)} %refs_0_.3, bf16[2,1024,2560]{2,1,0:T(8,128)(2,1)} %refs_1_.3, bf16[2,2560,1024]{2,1,0:T(8,128)(2,1)} %refs_2_.3), custom_call_target="tpu_custom_call" | custom-call | flops 32212254720 | bytes 57671680 | tf_op jit(solution)/shard_map/fwd0/pallas_call | solution.py:96
  54.4 116.2 %layer1.1 = (bf16[3,1024,2560]{2,1,0:T(8,128)(2,1)}, bf16[2048,1024]{1,0:T(8,128)(2,1)}) custom-call(bf16[2048,1024]{1,0:T(8,128)(2,1)} %get-tuple-element.25.h_ref, bf16[2048,1024]{1,0:T(8,128)(2,1)} %bitcast.11, bf16[2,1024,2560]{2,1,0:T(8,128)(2,1)} %refs_0_.3, bf16[2,1024,2560]{2,1,0:T(8,128)(2,1)} %refs_1_.3, bf16[2,2560,1024]{2,1,0:T(8,128)(2,1)} %refs_2_.3), custom_call_target="tpu_custom_call" | custom-call | flops 85899345920 | bytes 44040192 | tf_op jit(solution)/shard_map/layer1/pallas_call | solution.py:187
  170.5 0.0 reduce-scatter.3.cloned.1.call-update
  170.6 0.2 reduce-scatter.5.cloned.1.call-start
  170.8 70.1 %back0.1 = bf16[3,1024,2560]{2,1,0:T(8,128)(2,1)} custom-call(bf16[2048,1024]{1,0:T(8,128)(2,1)} %bitcast.13, bf16[2048,1024]{1,0:T(8,128)(2,1)} %get-tuple-element.26.dh_ref, f32[2048,2560]{1,0:T(8,128)} %get-tuple-element.27.gate_ref, f32[2048,2560]{1,0:T(8,128)} %get-tuple-element.28.up_ref, bf16[2,2560,1024]{2,1,0:T(8,128)(2,1)} %refs_2_.3), custom_call_target="tpu_custom_call" | custom-call | flops 42949672960 | bytes 62914560 | tf_op jit(solution)/shard_map/back0/pallas_call | solution.py:226
  240.9 36.6 %reduce-scatter.3.cloned.1.call-done = bf16[192,2560]{1,0:T(8,128)(2,1)} async-done(((bf16[3072,2560]{1,0:T(8,128)(2,1)}), bf16[192,2560]{1,0:T(8,128)(2,1)}) %reduce-scatter.3.cloned.1.call-update) | async-done | bytes 983056 | tf_op jit(solution)/shard_map/reduce_scatter | solution.py:285
  277.4 0.0 copy-start
  277.4 0.0 reduce-scatter.5.cloned.1.call-update
  277.5 0.0 all-gather.5.cloned.1.call-start
  277.5 0.7 all-gather.5.cloned.1.call-update
  278.2 0.0 all-gather.3.cloned.1.call-start
  278.2 108.4 %reduce-scatter.5.cloned.1.call-done = bf16[192,2560]{1,0:T(8,128)(2,1)} async-done(((bf16[3072,2560]{1,0:T(8,128)(2,1)}), bf16[192,2560]{1,0:T(8,128)(2,1)}) %reduce-scatter.5.cloned.1.call-update) | async-done | bytes 983056 | tf_op jit(solution)/shard_map/reduce_scatter | solution.py:288
  386.6 0.0 all-gather.3.cloned.1.call-update
  386.6 0.0 copy-done
  386.7 1.1 multiply_reduce_fusion
  387.8 2.3 multiply_reduce_fusion.1
  391.4 32.3 %psum.7 = f32[]{:T(128)} all-reduce(f32[]{:T(128)S(6)} %add.12), channel_id=1, replica_groups=mesh['rep'=1,'dp'=16] {'dp'}, use_global_device_ids=true, to_apply=%region_4.0 | all-reduce | flops 1 | bytes 8 | tf_op jit(solution)/shard_map/psum | solution.py:289
  424.4 38.1 %all-gather.5.cloned.1.call-done = bf16[3072,2560]{1,0:T(8,128)(2,1)} async-done(((bf16[192,2560]{1,0:T(8,128)(2,1)}), bf16[3072,2560]{1,0:T(8,128)(2,1)}) %all-gather.5.cloned.1.call-update) | async-done | bytes 15728656 | tf_op jit(solution)/shard_map/all_gather | solution.py:291
  462.5 56.9 %adamw1.1 = (bf16[2,1024,2560]{2,1,0:T(8,128)(2,1)}, bf16[2,1024,2560]{2,1,0:T(8,128)(2,1)}, bf16[2,2560,1024]{2,1,0:T(8,128)(2,1)}, f32[2,1024,2560]{2,1,0:T(8,...) custom-call(f32[1,1]{1,0:T(1,128)} %bitcast.4.f_ref, ...), custom_call_target="tpu_custom_call" | custom-call | flops 78643200 | bytes 173015040 | tf_op jit(solution)/shard_map/adamw1/pallas_call | solution.py:266
  519.3 17.8 %all-gather.3.cloned.1.call-done = bf16[3072,2560]{1,0:T(8,128)(2,1)} async-done(((bf16[192,2560]{1,0:T(8,128)(2,1)}), bf16[3072,2560]{1,0:T(8,128)(2,1)}) %all-gather.3.cloned.1.call-update) | async-done | bytes 15728656 | tf_op jit(solution)/shard_map/all_gather | solution.py:292
  537.1 56.9 %adamw0.1 = (bf16[2,1024,2560]{2,1,0:T(8,128)(2,1)}, bf16[2,1024,2560]{2,1,0:T(8,128)(2,1)}, bf16[2,2560,1024]{2,1,0:T(8,128)(2,1)}, f32[2,1024,2560]{2,1,0:T(8,...) custom-call(f32[1,1]{1,0:T(1,128)} %bitcast.4.f_ref, ...), custom_call_target="tpu_custom_call", output_to_operand_aliasing={{0}: (11, {}), {1}: (12, {}), {2}: (13, {}), {3}: (14, {}),... | custom-call | flops 78643200 | bytes 173015040 | tf_op jit(solution)/shard_map/adamw0/pallas_call | solution.py:266
Async XLA Ops:
  7.2 270.3 %reduce-scatter.3.cloned.1.call-start = ((), (), s32[]{:S(2)}) async-start(), calls=%async_computation.2 | async-start | bytes 16711680 | tf_op jit(solution)/shard_map/reduce_scatter | solution.py:285
  170.6 216.1 %reduce-scatter.5.cloned.1.call-start = ((), (), s32[]{:S(2)}) async-start(), calls=%async_computation.3 | async-start | bytes 16711680 | tf_op jit(solution)/shard_map/reduce_scatter | solution.py:288
  277.4 109.2 %copy-start = (bf16[192,2560]{1,0:T(8,128)(2,1)S(1)}, bf16[192,2560]{1,0:T(8,128)(2,1)}, u32[]{:S(2)}) copy-start(bf16[192,2560]{1,0:T(8,128)(2,1)} %reduce-scatter.3.cloned.1.call-done) | copy-start | bytes 2949124
  277.5 185.0 %all-gather.5.cloned.1.call-start = ((), (), s32[]{:S(2)}) async-start(), calls=%async_computation.5 | async-start | bytes 16711680 | tf_op jit(solution)/shard_map/all_gather | solution.py:291
  278.2 258.9 %all-gather.3.cloned.1.call-start = ((), (), s32[]{:S(2)}) async-start(), calls=%async_computation.4 | async-start | bytes 16711680 | tf_op jit(solution)/shard_map/all_gather | solution.py:292
Sparse Core Ops, SparseCore 0:
  170.7 106.7 reduce-scatter.2
  282.7 103.8 reduce-scatter.4
  388.9 73.5 all-gather.4
  464.6 72.5 all-gather.2

commit v2 on v1

v2 whole, which is shorter than its diff:
```python
import functools
import jax
import jax.numpy as jnp
from jax import lax
from jax.experimental import pallas as pl
from jax.experimental.pallas import tpu as pltpu
from jax.sharding import PartitionSpec as P

T, D, F = 2048, 1024, 2560
FT = 512
NT = F // FT
MB = 512
BF, F32 = jnp.bfloat16, jnp.float32
VL = 64 * 1024 * 1024 - 128 * 1024
NN = (((1,), (0,)), ((), ()))
NTR = (((1,), (1,)), ((), ()))


def dot(a, b, dims=NN):
    return lax.dot_general(a, b, dims, preferred_element_type=F32)


def params(**more):
    return pltpu.CompilerParams(vmem_limit_bytes=VL, dimension_semantics=("arbitrary",), **more)


def norm_block(h):
    wide = h.astype(F32)
    scale = lax.rsqrt(jnp.mean(wide * wide, -1, keepdims=True) + 1e-6)
    return (wide * scale).astype(BF)


def rows(i, n):
    return pl.ds(pl.multiple_of(i * n, n), n)


def norm_into(h_ref, a_ref, at_ref, n=256):
    def body(i, _):
        a = norm_block(h_ref[rows(i, n), :])
        if a_ref is not None:
            a_ref[rows(i, n), :] = a
        if at_ref is not None:
            at_ref[:, rows(i, n)] = a.T
        return 0
    lax.fori_loop(0, T // n, body, 0)


def transpose_into(h_ref, at_ref, n=256):
    def body(i, _):
        at_ref[:, rows(i, n)] = h_ref[rows(i, n), :].T
        return 0
    lax.fori_loop(0, T // n, body, 0)


def kernel_a(x_ref, wg_ref, wu_ref, wd_ref, gate_ref, up_ref, h1_ref, at_ref, a_ref, acc_ref):
    t = pl.program_id(0)

    @pl.when(t == 0)
    def _():
        norm_into(x_ref, a_ref, at_ref)

    def body(first, i, _):
        r = rows(i, MB)
        a = a_ref[r, :]
        gate = dot(a, wg_ref[0])
        up = dot(a, wu_ref[0])
        gate_ref[r, :] = gate
        up_ref[r, :] = up
        hid = (gate * jax.nn.sigmoid(gate) * up).astype(BF)
        y = dot(hid, wd_ref[0])
        if first:
            acc_ref[r, :] = y
        else:
            acc_ref[r, :] += y
        return 0

    @pl.when(t == 0)
    def _():
        lax.fori_loop(0, T // MB, functools.partial(body, True), 0)

    @pl.when(t > 0)
    def _():
        lax.fori_loop(0, T // MB, functools.partial(body, False), 0)

    @pl.when(t == NT - 1)
    def _():
        def fin(i, _):
            r = rows(i, MB)
            h1_ref[r, :] = (x_ref[r, :].astype(F32) + acc_ref[r, :].astype(BF).astype(F32)).astype(BF)
            return 0
        lax.fori_loop(0, T // MB, fin, 0)


def forward0(x, wg, wu, wd):
    whole = pl.BlockSpec((T, D), lambda t: (0, 0), pipeline_mode=pl.Buffered(1))
    return pl.pallas_call(
        kernel_a,
        grid=(NT,),
        in_specs=[whole,
                  pl.BlockSpec((1, D, FT), lambda t: (0, 0, t)),
                  pl.BlockSpec((1, D, FT), lambda t: (0, 0, t)),
                  pl.BlockSpec((1, FT, D), lambda t: (0, t, 0))],
        out_specs=[pl.BlockSpec((T, FT), lambda t: (0, t)), pl.BlockSpec((T, FT), lambda t: (0, t)), whole,
                   pl.BlockSpec((D, T), lambda t: (0, 0), pipeline_mode=pl.Buffered(1))],
        out_shape=[jax.ShapeDtypeStruct((T, F), F32), jax.ShapeDtypeStruct((T, F), F32), jax.ShapeDtypeStruct((T, D), BF),
                   jax.ShapeDtypeStruct((D, T), BF)],
        scratch_shapes=[pltpu.VMEM((T, D), BF), pltpu.VMEM((T, D), F32)],
        compiler_params=params(),
        cost_estimate=pl.CostEstimate(flops=6 * T * D * F, bytes_accessed=8 * T * F + 6 * D * F, transcendentals=0),
        name="fwd0",
    )(x, wg, wu, wd)


def back_elementwise(gate, up, dhid):
    s = jax.nn.sigmoid(gate)
    silu = gate * s
    dh = dhid.astype(BF).astype(F32)
    hid = (silu * up).astype(BF)
    du = (dh * silu).astype(BF)
    dg = (dh * up * (s + silu * (1.0 - s))).astype(BF)
    return hid, dg, du


def weight_grads(at_ref, dt_ref, hid_ref, dg_ref, du_ref, g_ref, slot, lo, hi):
    def body(n, _):
        r = rows(n, 256)
        at = at_ref[r, :]
        g_ref[slot, 0, r, :] = dot(at, dg_ref[...]).astype(BF)
        g_ref[slot, 1, r, :] = dot(at, du_ref[...]).astype(BF)
        g_ref[slot, 2, r, :] = dot(dt_ref[r, :], hid_ref[...]).astype(BF)
        return 0
    lax.fori_loop(lo, hi, body, 0)


CORE = 1
ORDER = ((8, 4, 2), (4, 2, 8), (2, 8, 4))
PARTNERS = (1, 2, 4, 8)
HALVES = (512, 256, 128, 64)


def bit(stride):
    return (lax.axis_index("dp") // stride) % 2


def partner(stride):
    return {"dp": lax.axis_index("dp") + stride * (1 - 2 * bit(stride))}


def greet():
    barrier = pltpu.get_barrier_semaphore()
    for stride in PARTNERS:
        pl.semaphore_signal(barrier, inc=1, device_id=partner(stride), device_id_type=pl.DeviceIdType.MESH)
    pl.semaphore_wait(barrier, len(PARTNERS))


def some(start, n):
    return pl.ds(pl.multiple_of(start, 64), n)


def strides(c):
    return (CORE,) + ORDER[c]


class Scatter:
    def __init__(self, g, got, sent, send_sem, recv_sem):
        self.g, self.got, self.sent, self.send_sem, self.recv_sem = g, got, sent, send_sem, recv_sem

    def total(self, slot, c, stage, own):
        bits = [bit(s) for s in strides(c)]
        n = HALVES[stage] if stage < 4 else 64
        last = bits[stage] if own else 1 - bits[stage]
        keep = bits[:stage] + [last]
        start = sum(b * HALVES[i] for i, b in enumerate(keep))
        out = self.g[slot, c, some(start, n), :].astype(F32)
        for i in range(stage):
            start = sum(b * HALVES[j] for j, b in enumerate(keep) if j > i)
            out = out + self.got[i][slot, c, some(start, n), :].astype(F32)
        return out

    def copy(self, slot, c, stage):
        n = HALVES[stage]
        src = self.g.at[slot, c, some((1 - bit(CORE)) * 512, 512), :] if stage == 0 else self.sent[stage - 1].at[slot, c]
        return pltpu.make_async_remote_copy(
            src_ref=src, dst_ref=self.got[stage].at[slot, c], send_sem=self.send_sem.at[stage, c, slot], recv_sem=self.recv_sem.at[stage, c, slot],
            device_id=partner(strides(c)[stage]), device_id_type=pl.DeviceIdType.MESH)

    def begin(self, slot):
        for c in range(3):
            self.copy(slot, c, 0).start()

    def advance(self, slot, stage):
        for c in range(3):
            self.copy(slot, c, stage - 1).wait_recv()
            self.sent[stage - 1][slot, c] = self.total(slot, c, stage, False).astype(BF)
            self.copy(slot, c, stage).start()

    def finish(self, slot, shard, squares_ref):
        for c in range(3):
            self.copy(slot, c, 3).wait_recv()
            bits = [bit(s) for s in strides(c)]
            start = sum(b * HALVES[i] for i, b in enumerate(bits))
            out = self.g[slot, c, some(start, 64), :].astype(F32)
            for i in range(4):
                start = sum(b * HALVES[j] for j, b in enumerate(bits) if j > i)
                out = out + self.got[i][slot, c, some(start, 64), :].astype(F32)
            out = out.astype(BF)
            shard[c] = out
            squares = out.astype(F32) * out.astype(F32)
            squares_ref[...] += sum(squares[8 * i:8 * i + 8, 128 * j:128 * j + 128] for i in range(8) for j in range(FT // 128))
            for stage in range(4):
                self.copy(slot, c, stage).wait_send()


class Gather:
    def __init__(self, shards, full, own_sem, send_sem, recv_sem):
        self.shards, self.full, self.own_sem, self.send_sem, self.recv_sem = shards, full, own_sem, send_sem, recv_sem

    def place(self, tile, c, n):
        start = sum(bit(s) * HALVES[i] for i, s in enumerate(strides(c)) if HALVES[i] >= n)
        return self.full.at[c, some(start, n), pl.ds(pl.multiple_of(tile * FT, FT), FT)]

    def own(self, tile, c):
        return pltpu.make_async_copy(self.shards.at[tile, c], self.place(tile, c, 64), self.own_sem.at[tile, c])

    def copy(self, tile, c, stage):
        place = self.place(tile, c, 64 << stage)
        return pltpu.make_async_remote_copy(
            src_ref=self.shards.at[tile, c] if stage == 0 else place, dst_ref=place,
            send_sem=self.send_sem.at[tile, stage, c], recv_sem=self.recv_sem.at[tile, stage, c],
            device_id=partner(strides(c)[3 - stage]), device_id_type=pl.DeviceIdType.MESH)

    def begin(self, tile):
        for c in range(3):
            self.own(tile, c).start()
            self.copy(tile, c, 0).start()

    def advance(self, tile, stage):
        for c in range(3):
            if stage == 1:
                self.own(tile, c).wait()
            self.copy(tile, c, stage - 1).wait_recv()
            self.copy(tile, c, stage).start()

    def finish(self, tile):
        for c in range(3):
            self.copy(tile, c, 3).wait_recv()
            for stage in range(4):
                self.copy(tile, c, stage).wait_send()


def gather_scratch(tiles):
    return [pltpu.SemaphoreType.DMA((tiles, 3)), pltpu.SemaphoreType.DMA((tiles, 4, 3)), pltpu.SemaphoreType.DMA((tiles, 4, 3))]


def scatter_scratch(slots):
    return ([pltpu.VMEM((slots, 3, D, FT), BF)] + [pltpu.VMEM((slots, 3, n, FT), BF) for n in HALVES]
            + [pltpu.VMEM((slots, 3, n, FT), BF) for n in HALVES[1:]]
            + [pltpu.SemaphoreType.DMA((4, 3, slots)), pltpu.SemaphoreType.DMA((4, 3, slots))])


def scatter_of(refs):
    return Scatter(refs[0], refs[1:5], refs[5:8], refs[8], refs[9])


EARLY = 3


def kernel_b(h_hbm, dy_hbm, wg_ref, wu_ref, wd_ref, full_hbm, late_hbm, squares_ref, dh_hbm, dht_hbm,
             a_ref, dy_ref, at_ref, dt_ref, accg_ref, accu_ref, hid_ref, dg_ref, du_ref, sem, shard_ref, *rest):
    t = pl.program_id(0)
    s = scatter_of(rest[:10])
    g = Gather(shard_ref, full_hbm, *rest[10:])
    store_late = pltpu.make_async_copy(shard_ref.at[pl.ds(EARLY, NT - EARLY)], late_hbm, sem.at[4])
    load_h = pltpu.make_async_copy(h_hbm, a_ref, sem.at[0])
    load_dy = pltpu.make_async_copy(dy_hbm, dy_ref, sem.at[1])
    store_dh = pltpu.make_async_copy(dy_ref, dh_hbm, sem.at[2])
    store_dht = pltpu.make_async_copy(dt_ref, dht_hbm, sem.at[3])
    now, before = t % 2, (t + 1) % 2

    @pl.when(t == 0)
    def _():
        load_h.start()
        load_dy.start()
        greet()
        squares_ref[...] = jnp.zeros_like(squares_ref)
        load_h.wait()
        norm_into(a_ref, a_ref, at_ref)
        load_dy.wait()
        transpose_into(dy_ref, dt_ref)

    def body(first, i, _):
        r = rows(i, MB)
        a = a_ref[r, :]
        gate = dot(a, wg_ref[0])
        up = dot(a, wu_ref[0])
        dhid = dot(dy_ref[r, :], wd_ref[0], NTR)
        hid, dg, du = back_elementwise(gate, up, dhid)
        hid_ref[r, :] = hid
        dg_ref[r, :] = dg
        du_ref[r, :] = du
        yg = dot(dg, wg_ref[0], NTR)
        yu = dot(du, wu_ref[0], NTR)
        if first:
            accg_ref[r, :] = yg
            accu_ref[r, :] = yu
        else:
            accg_ref[r, :] += yg
            accu_ref[r, :] += yu
        return 0

    def half(lo):
        @pl.when(t == 0)
        def _():
            lax.fori_loop(lo, lo + 2, functools.partial(body, True), 0)

        @pl.when((t > 0) & (t < NT))
        def _():
            lax.fori_loop(lo, lo + 2, functools.partial(body, False), 0)

    def advance(stage):
        @pl.when(t > 0)
        def _():
            s.advance(before, stage)

    def grads(lo):
        @pl.when(t < NT)
        def _():
            weight_grads(at_ref, dt_ref, hid_ref, dg_ref, du_ref, s.g, now, lo, lo + 2)

    def collect(stage, behind):
        @pl.when((t >= behind) & (t < behind + EARLY))
        def _():
            if stage == 4:
                g.finish(t - behind)
            else:
                g.advance(t - behind, stage)

    half(0)
    collect(3, 3)
    advance(1)
    collect(1, 2)
    half(2)

    @pl.when(t == NT - 1)
    def _():
        load_h.start()

    advance(2)
    grads(0)

    @pl.when(t == NT)
    def _():
        load_h.wait()

        def fin(i, _):
            r = rows(i, 256)
            wide = a_ref[r, :].astype(F32)
            scale = lax.rsqrt(jnp.mean(wide * wide, -1, keepdims=True) + 1e-6)
            da = (accg_ref[r, :].astype(BF).astype(F32) + accu_ref[r, :].astype(BF).astype(F32)).astype(BF).astype(F32)
            inner = jnp.mean(da * wide, -1, keepdims=True)
            dn = (da * scale - wide * (scale * scale * scale * inner)).astype(BF).astype(F32)
            dh = (dy_ref[r, :].astype(F32) + dn).astype(BF)
            dy_ref[r, :] = dh
            dt_ref[:, r] = dh.T
            return 0
        lax.fori_loop(0, T // 256, fin, 0)
        store_dh.start()
        store_dht.start()

    advance(3)
    collect(2, 2)
    collect(4, 3)
    grads(2)

    @pl.when(t > 0)
    def _():
        s.finish(before, shard_ref.at[jnp.maximum(t - 1, 0)], squares_ref)

    @pl.when((t >= 1) & (t < 1 + EARLY))
    def _():
        g.begin(t - 1)

    @pl.when(t < NT)
    def _():
        s.begin(now)

    @pl.when(t == NT)
    def _():
        store_late.start()
        store_dh.wait()
        store_dht.wait()
        store_late.wait()


def layer1(h1, dy, wg, wu, wd):
    any_ = pl.BlockSpec(memory_space=pl.ANY)
    at = lambda t: jnp.minimum(t, NT - 1)
    return pl.pallas_call(
        kernel_b,
        grid=(NT + 1,),
        in_specs=[any_, any_,
                  pl.BlockSpec((1, D, FT), lambda t: (1, 0, at(t))),
                  pl.BlockSpec((1, D, FT), lambda t: (1, 0, at(t))),
                  pl.BlockSpec((1, FT, D), lambda t: (1, at(t), 0))],
        out_specs=[any_, any_, pl.BlockSpec((8, 128), lambda t: (0, 0)), any_, any_],
        out_shape=[jax.ShapeDtypeStruct((3, D, EARLY * FT), BF), jax.ShapeDtypeStruct((NT - EARLY, 3, 64, FT), BF),
                   jax.ShapeDtypeStruct((8, 128), F32), jax.ShapeDtypeStruct((T, D), BF), jax.ShapeDtypeStruct((D, T), BF)],
        scratch_shapes=[pltpu.VMEM((T, D), BF), pltpu.VMEM((T, D), BF), pltpu.VMEM((D, T), BF), pltpu.VMEM((D, T), BF),
                        pltpu.VMEM((T, D), F32), pltpu.VMEM((T, D), F32),
                        pltpu.VMEM((T, FT), BF), pltpu.VMEM((T, FT), BF), pltpu.VMEM((T, FT), BF), pltpu.SemaphoreType.DMA((5,)),
                        pltpu.VMEM((NT, 3, 64, FT), BF)]
        + scatter_scratch(2) + gather_scratch(EARLY),
        compiler_params=params(collective_id=1, has_side_effects=True),
        cost_estimate=pl.CostEstimate(flops=16 * T * D * F, bytes_accessed=12 * D * F + 6 * T * D, transcendentals=0),
        name="layer1",
    )(h1, dy, wg, wu, wd)


def kernel_c(at_ref, dh_ref, dt_ref, gate_ref, up_ref, wd_ref, late_ref, squares1_ref, shard_ref, full_hbm, factor_ref,
             hid_ref, dg_ref, du_ref, squares_ref, xs, xr, x_send, x_recv, *rest):
    t = pl.program_id(0)
    s = scatter_of(rest[:10])
    gat = Gather(late_ref, full_hbm, *rest[10:])

    def collect(step, stage):
        @pl.when(t == step)
        def _():
            for tile in range(NT - EARLY):
                if stage == 0:
                    gat.begin(tile)
                elif stage == 4:
                    gat.finish(tile)
                else:
                    gat.advance(tile, stage)

    now, one, two = t % 3, (t + 2) % 3, (t + 1) % 3

    @pl.when(t == 0)
    def _():
        greet()
        squares_ref[...] = squares1_ref[...]

    collect(0, 0)

    @pl.when(t < NT)
    def _():
        def body(i, _):
            r = rows(i, MB)
            dhid = dot(dh_ref[r, :], wd_ref[0], NTR)
            hid, dg, du = back_elementwise(gate_ref[r, :], up_ref[r, :], dhid)
            hid_ref[r, :] = hid
            dg_ref[r, :] = dg
            du_ref[r, :] = du
            return 0
        lax.fori_loop(0, T // MB, body, 0)

    def grads(lo):
        @pl.when(t < NT)
        def _():
            weight_grads(at_ref, dt_ref, hid_ref, dg_ref, du_ref, s.g, now, lo, lo + 2)

    @pl.when(t >= 2)
    def _():
        s.advance(two, 3)

    @pl.when((t >= 1) & (t <= NT))
    def _():
        s.advance(one, 1)

    collect(0, 1)
    collect(2, 4)
    grads(0)

    @pl.when(t >= 2)
    def _():
        s.finish(two, shard_ref, squares_ref)

    collect(0, 2)
    collect(1, 3)
    grads(2)

    @pl.when(t < NT)
    def _():
        s.begin(now)

    @pl.when((t >= 1) & (t <= NT))
    def _():
        s.advance(one, 2)

    @pl.when(t == NT + 1)
    def _():
        total = squares_ref[...]
        for k, stride in enumerate(PARTNERS):
            xs[k] = total
            copy = pltpu.make_async_remote_copy(src_ref=xs.at[k], dst_ref=xr.at[k], send_sem=x_send.at[k], recv_sem=x_recv.at[k],
                                                device_id=partner(stride), device_id_type=pl.DeviceIdType.MESH)
            copy.start()
            copy.wait()
            total = total + xr[k]
        total = jnp.sum(jnp.sum(total, 0, keepdims=True), 1, keepdims=True)
        factor_ref[...] = jnp.broadcast_to(jnp.minimum(1.0, 0.5 * lax.rsqrt(total / (6 * D * F) + 1e-30)), (8, 128))


def back0(at0, dh1, dht1, gate, up, wd, late, squares1):
    whole = pl.BlockSpec((T, D), lambda t: (0, 0), pipeline_mode=pl.Buffered(1))
    turned = pl.BlockSpec((D, T), lambda t: (0, 0), pipeline_mode=pl.Buffered(1))
    at = lambda t: jnp.minimum(t, NT - 1)
    return pl.pallas_call(
        kernel_c,
        grid=(NT + 2,),
        in_specs=[turned, whole, turned, pl.BlockSpec((T, FT), lambda t: (0, at(t))), pl.BlockSpec((T, FT), lambda t: (0, at(t))),
                  pl.BlockSpec((1, FT, D), lambda t: (0, at(t), 0)),
                  pl.BlockSpec((NT - EARLY, 3, 64, FT), lambda t: (0, 0, 0, 0)), pl.BlockSpec((8, 128), lambda t: (0, 0))],
        out_specs=[pl.BlockSpec((3, 64, FT), lambda t: (0, 0, jnp.maximum(t - 2, 0))), pl.BlockSpec(memory_space=pl.ANY),
                   pl.BlockSpec((8, 128), lambda t: (0, 0))],
        out_shape=[jax.ShapeDtypeStruct((3, 64, F), BF), jax.ShapeDtypeStruct((3, D, (NT - EARLY) * FT), BF), jax.ShapeDtypeStruct((8, 128), F32)],
        scratch_shapes=[pltpu.VMEM((T, FT), BF), pltpu.VMEM((T, FT), BF), pltpu.VMEM((T, FT), BF), pltpu.VMEM((8, 128), F32),
                        pltpu.VMEM((4, 8, 128), F32), pltpu.VMEM((4, 8, 128), F32), pltpu.SemaphoreType.DMA((4,)), pltpu.SemaphoreType.DMA((4,))]
        + scatter_scratch(3) + gather_scratch(NT - EARLY),
        compiler_params=params(collective_id=2, has_side_effects=True),
        cost_estimate=pl.CostEstimate(flops=8 * T * D * F, bytes_accessed=8 * T * F + 8 * D * F, transcendentals=0),
        name="back0",
    )(at0, dh1, dht1, gate, up, wd, late, squares1)


FB = 256


def adamw(w, m, v, g):
    m = 0.9 * m + 0.1 * g
    v = 0.95 * v + 0.05 * g * g
    w = w.astype(F32)
    return (w - 0.02 * (m * lax.rsqrt(v + 1e-8) + 0.1 * w)).astype(BF), m, v


def update(refs, outs, i, where, g):
    at = (0,) + where
    new = adamw(refs[i][at], refs[3 + i][at], refs[6 + i][at], g)
    for k in range(3):
        outs[3 * k + i][at] = new[k]


def kernel_o1(f_ref, early_ref, late_ref, *refs):
    ins, outs = refs[:9], refs[-9:]
    factor = f_ref[0:1, 0:1]

    def run(g_ref):
        for i in range(3):
            g = g_ref[i].astype(F32)
            update(ins, outs, i, (slice(None), slice(None)), (g.T if i == 2 else g) * factor)

    early = EARLY * FT // FB

    @pl.when(pl.program_id(0) < early)
    def _():
        run(early_ref)

    @pl.when(pl.program_id(0) >= early)
    def _():
        run(late_ref)


def owner(c, k):
    return sum(s * (k * 64 // HALVES[i] % 2) for i, s in enumerate(strides(c)))


def kernel_o0(f_ref, g_ref, *refs):
    ins, outs = refs[:9], refs[-9:]
    factor = f_ref[0:1, 0:1]
    for k in range(8):
        both = slice(128 * k, 128 * k + 128)
        for i in range(3):
            g = jnp.concatenate([g_ref[owner(i, 2 * k + half), i] for half in range(2)], 0).astype(F32)
            where = (slice(None), both) if i == 2 else (both, slice(None))
            update(ins, outs, i, where, (g.T if i == 2 else g) * factor)


def optimizer(layer, kernel, factor, gradients, specs, arrays, before):
    wide = pl.BlockSpec((1, D, FB), lambda t: (layer, 0, t))
    tall = pl.BlockSpec((1, FB, D), lambda t: (layer, t, 0))
    three = [wide, wide, tall]
    first = 1 + len(gradients) + 9
    return pl.pallas_call(
        kernel,
        grid=(F // FB,),
        in_specs=[pl.BlockSpec((8, 128), lambda t: (0, 0))] + specs + three * 3 + [pl.BlockSpec(memory_space=pl.ANY)] * len(before),
        out_specs=three * 3,
        out_shape=[jax.ShapeDtypeStruct(a.shape, a.dtype) for a in arrays],
        input_output_aliases={first + i: i for i in range(len(before))},
        compiler_params=params(),
        cost_estimate=pl.CostEstimate(flops=30 * D * F, bytes_accessed=66 * D * F, transcendentals=3 * D * F),
        name=f"adamw{layer}",
    )(factor, *gradients, *arrays, *before)


def solution(mesh):
    def step(x, dy, *arrays):
        wg, wu, wd = arrays[:3]
        gate, up, h1, at0 = forward0(x[0], wg, wu, wd)
        early, late, squares1, dh1, dht1 = layer1(h1, dy[0], wg, wu, wd)
        s0, rest, factor = back0(at0, dh1, dht1, gate, up, wd, late, squares1)
        full0 = lax.all_gather(s0, "dp")
        n = EARLY * FT // FB
        specs = [pl.BlockSpec((3, D, FB), lambda t: (0, 0, jnp.minimum(t, n - 1))),
                 pl.BlockSpec((3, D, FB), lambda t: (0, 0, jnp.maximum(t - n, 0)))]
        new = optimizer(1, kernel_o1, factor, (early, rest), specs, arrays, ())
        specs = [pl.BlockSpec((16, 3, 64, FB), lambda t: (0, 0, 0, t))]
        return tuple(optimizer(0, kernel_o0, factor, (full0,), specs, arrays, new))

    return jax.shard_map(
        step,
        mesh=mesh,
        in_specs=(P(("rep", "dp"), None, None),) * 2 + (P(None, None, None),) * 9,
        out_specs=(P("rep", None, None),) * 9,
        check_vma=False,
    )
```

time: 601 us -> 446 us (0.74)
  waiting for transfers between devices: 202 us -> 4.6 us
  Pallas kernels: 347 us -> 427 us
  blocking collectives: 32.3 us -> 0 us
    reduce_scatter x2 -> x0, waiting for transfers between devices: 145 us -> none  [the longest x1 108 us: step(): lax.psum_scatter(g0.reshape(3 * D, F), 'dp', scatter_dimension=0, tiled=T...]
    pallas_call x4, Pallas kernels: 300 us -> 377 us  [the longest x1 145 us: layer1(): pl.pallas_call(kernel_b, grid=(NT + 1,), in_specs=[any_, any_, pl.BlockSp...]
    all_gather x2 -> x1, waiting for transfers between devices: 55.9 us -> 4.58 us  [step(): full0 = lax.all_gather(s0, 'dp')]
    psum x1 -> x0, blocking collectives: 32.3 us -> none  [step(): lax.psum(sum((jnp.sum(s.astype(F32) ** 2) for s in (s0, s1))), 'dp')]
  transfers between devices with their start and end apart: 4 -> 1, of which waited for: 4 -> 1; matrix products, arithmetic and copies ran while one was open for 1% -> 0% of each run, Pallas kernels for 21% -> 15%
where the time goes in v2:
time: 446 us
  Pallas kernels  427 us (96%)
  between operations  14.1 us (3%)
  waiting for transfers between devices  4.6 us (1%)
    pallas_call x1, Pallas kernels, layer1(): pl.pallas_call(kernel_b, grid=(NT + 1,), in_specs=[any_, any_, pl.BlockSp...  145 us
    pallas_call x2, Pallas kernels, optimizer(): pl.pallas_call(kernel, grid=(F // FB,), in_specs=[pl.BlockSpec((8, 128),...  125 us
    pallas_call x1, Pallas kernels, back0(): pl.pallas_call(kernel_c, grid=(NT + 2,), in_specs=[turned, whole, turned,...  107 us
    pallas_call x1, Pallas kernels, forward0(): pl.pallas_call(kernel_a, grid=(NT,), in_specs=[whole, pl.BlockSpec((1, D,...  49.5 us
  transfers between devices with their start and end apart: 1, of which 1 were waited for; matrix products, arithmetic and copies ran while one was open for 0% of the time, Pallas kernels for 15%

profile of v2, /device:TPU:0, one launch (start us, length us, event | category | flops | bytes accessed | tf_op | source)
XLA Modules:
  0.0 445.6 jit_solution(13395522479342356448)
XLA Ops:
  7.2 0.0 all-gather.3.cloned.1.call-start
  7.2 49.5 %fwd0.1 = (f32[2048,2560]{1,0:T(8,128)}, f32[2048,2560]{1,0:T(8,128)}, bf16[2048,1024]{1,0:T(8,128)(2,1)}, bf16[1024,2048]{1,0:T(8,128)(2,1)}) custom-call(bf16[2048,1024]{1,0:T(8,128)(2,1)} %bitcast.4, bf16[2,1024,2560]{2,1,0:T(8,128)(2,1)} %refs_0_.3, bf16[2,1024,2560]{2,1,0:T(8,128)(2,1)} %refs_1_.3, bf16[2,2560,1024]{2,1,0:T(8,128)(2,1)} %refs_2_.3), custom_call_target="tpu_custom_call" | custom-call | flops 32212254720 | bytes 57671680 | tf_op jit(solution)/shard_map/fwd0/pallas_call | solution.py:96
  56.8 145.0 %layer1.1 = (bf16[3,1024,1536]{2,1,0:T(8,128)(2,1)}, bf16[2,3,64,512]{3,2,1,0:T(8,128)(2,1)}, f32[8,128]{1,0:T(8,128)}, bf16[2048,1024]{1,0:T(8,128)(2,1)}, bf16[1024,2048]{1,0:T(8,128)(2,1)}) custom-call(bf16[2048,1024]{1,0:T(8,128)(2,1)} %get-tuple-element.31.h_hbm, bf16[2048,1024]{1,0:T(8,128)(2,1)} %bitcast.5, bf16[2,1024,2560]{2,1,0:T(8,128)(2,1)} %refs_0_.3, ...), custom_call_target="tpu_custom_call" | custom-call | flops 85899345920 | bytes 44040192 | tf_op jit(solution)/shard_map/layer1/pallas_call | solution.py:398
  201.8 107.0 %back0.1 = (bf16[3,64,2560]{2,1,0:T(8,128)(2,1)}, bf16[3,1024,1024]{2,1,0:T(8,128)(2,1)}, f32[8,128]{1,0:T(8,128)}) custom-call(bf16[1024,2048]{1,0:T(8,128)(2,1)} %get-tuple-element.30.at_ref, bf16[2048,1024]{1,0:T(8,128)(2,1)} %get-tuple-element.32.dh_ref, bf16[1024,2048]{1,0:T(8,128)(2,1)} %get-tuple-element.33.dt_ref, ...), custom_call_target="tpu_custom_call" | custom-call | flops 42949672960 | bytes 62914560 | tf_op jit(solution)/shard_map/back0/pallas_call | solution.py:508
  308.8 0.0 all-gather.3.cloned.1.call-update
  308.9 67.8 %adamw1.1 = (bf16[2,1024,2560]{2,1,0:T(8,128)(2,1)}, bf16[2,1024,2560]{2,1,0:T(8,128)(2,1)}, bf16[2,2560,1024]{2,1,0:T(8,128)(2,1)}, f32[2,1024,2560]{2,1,0:T(8,...) custom-call(f32[8,128]{1,0:T(8,128)} %get-tuple-element.38.f_ref, ...), custom_call_target="tpu_custom_call" | custom-call | flops 78643200 | bytes 173015040 | tf_op jit(solution)/shard_map/adamw1/pallas_call | solution.py:583
  376.7 4.6 %all-gather.3.cloned.1.call-done = bf16[48,64,2560]{2,1,0:T(8,128)(2,1)} async-done(((bf16[3,64,2560]{2,1,0:T(8,128)(2,1)}), bf16[48,64,2560]{2,1,0:T(8,128)(2,1)}) %all-gather.3.cloned.1.call-update) | async-done | bytes 15728656 | tf_op jit(solution)/shard_map/all_gather | solution.py:602
  381.3 57.5 %adamw0.1 = (bf16[2,1024,2560]{2,1,0:T(8,128)(2,1)}, bf16[2,1024,2560]{2,1,0:T(8,128)(2,1)}, bf16[2,2560,1024]{2,1,0:T(8,128)(2,1)}, f32[2,1024,2560]{2,1,0:T(8,...) custom-call(f32[8,128]{1,0:T(8,128)} %get-tuple-element.38.f_ref, ...), custom_call_target="tpu_custom_call", output_to_operand_aliasing={{0}: (11, {}), {1}: (12, {}), {2}: (13, {}), {3}: (14, {}),... | custom-call | flops 78643200 | bytes 173015040 | tf_op jit(solution)/shard_map/adamw0/pallas_call | solution.py:583
Async XLA Ops:
  7.2 374.1 %all-gather.3.cloned.1.call-start = ((), (), s32[]{:S(2)}) async-start(), calls=%async_computation | async-start | bytes 16711680 | tf_op jit(solution)/shard_map/all_gather | solution.py:602
Sparse Core Ops, SparseCore 0:
  309.0 72.2 all-gather.2

commit v3 on v2

v3 whole, which is shorter than its diff:
```python
import functools
import jax
import jax.numpy as jnp
from jax import lax
from jax.experimental import pallas as pl
from jax.experimental.pallas import tpu as pltpu
from jax.sharding import PartitionSpec as P

T, D, F = 2048, 1024, 2560
FT = 512
NT = F // FT
MB = 512
BF, F32 = jnp.bfloat16, jnp.float32
VL = 64 * 1024 * 1024 - 128 * 1024
NN = (((1,), (0,)), ((), ()))
NTR = (((1,), (1,)), ((), ()))
TN = (((0,), (0,)), ((), ()))


def dot(a, b, dims=NN):
    return lax.dot_general(a, b, dims, preferred_element_type=F32)


def params(**more):
    return pltpu.CompilerParams(vmem_limit_bytes=VL, dimension_semantics=("arbitrary",), **more)


def norm_block(h):
    wide = h.astype(F32)
    scale = lax.rsqrt(jnp.mean(wide * wide, -1, keepdims=True) + 1e-6)
    return (wide * scale).astype(BF)


def rows(i, n):
    return pl.ds(pl.multiple_of(i * n, n), n)


def norm_into(h_ref, a_ref, n=256):
    def body(i, _):
        a_ref[rows(i, n), :] = norm_block(h_ref[rows(i, n), :])
        return 0
    lax.fori_loop(0, T // n, body, 0)


def kernel_a(x_ref, wg_ref, wu_ref, wd_ref, gate_ref, up_ref, h1_ref, a_ref, acc_ref):
    t = pl.program_id(0)

    @pl.when(t == 0)
    def _():
        norm_into(x_ref, a_ref)

    def body(first, i, _):
        r = rows(i, MB)
        a = a_ref[r, :]
        gate = dot(a, wg_ref[0])
        up = dot(a, wu_ref[0])
        gate_ref[r, :] = gate
        up_ref[r, :] = up
        hid = (gate * jax.nn.sigmoid(gate) * up).astype(BF)
        y = dot(hid, wd_ref[0])
        if first:
            acc_ref[r, :] = y
        else:
            acc_ref[r, :] += y
        return 0

    @pl.when(t == 0)
    def _():
        lax.fori_loop(0, T // MB, functools.partial(body, True), 0, unroll=2)

    @pl.when(t > 0)
    def _():
        lax.fori_loop(0, T // MB, functools.partial(body, False), 0, unroll=2)

    @pl.when(t == NT - 1)
    def _():
        def fin(i, _):
            r = rows(i, MB)
            h1_ref[r, :] = (x_ref[r, :].astype(F32) + acc_ref[r, :].astype(BF).astype(F32)).astype(BF)
            return 0
        lax.fori_loop(0, T // MB, fin, 0)


def forward0(x, wg, wu, wd):
    whole = pl.BlockSpec((T, D), lambda t: (0, 0), pipeline_mode=pl.Buffered(1))
    return pl.pallas_call(
        kernel_a,
        grid=(NT,),
        in_specs=[whole,
                  pl.BlockSpec((1, D, FT), lambda t: (0, 0, t)),
                  pl.BlockSpec((1, D, FT), lambda t: (0, 0, t)),
                  pl.BlockSpec((1, FT, D), lambda t: (0, t, 0))],
        out_specs=[pl.BlockSpec((T, FT), lambda t: (0, t)), pl.BlockSpec((T, FT), lambda t: (0, t)), whole, whole],
        out_shape=[jax.ShapeDtypeStruct((T, F), F32), jax.ShapeDtypeStruct((T, F), F32), jax.ShapeDtypeStruct((T, D), BF),
                   jax.ShapeDtypeStruct((T, D), BF)],
        scratch_shapes=[pltpu.VMEM((T, D), F32)],
        compiler_params=params(),
        cost_estimate=pl.CostEstimate(flops=6 * T * D * F, bytes_accessed=8 * T * F + 6 * D * F, transcendentals=0),
        name="fwd0",
    )(x, wg, wu, wd)


def back_elementwise(gate, up, dhid):
    s = jax.nn.sigmoid(gate)
    silu = gate * s
    dh = dhid.astype(BF).astype(F32)
    hid = (silu * up).astype(BF)
    du = (dh * silu).astype(BF)
    dg = (dh * up * (s + silu * (1.0 - s))).astype(BF)
    return hid, dg, du


def weight_grads(a_ref, d_ref, hid_ref, dg_ref, du_ref, g_ref, slot, n):
    r = rows(n, 512)
    g_ref[slot, 0, r, :] = dot(a_ref[:, r], dg_ref[...], TN).astype(BF)
    g_ref[slot, 1, r, :] = dot(a_ref[:, r], du_ref[...], TN).astype(BF)
    g_ref[slot, 2, r, :] = dot(d_ref[:, r], hid_ref[...], TN).astype(BF)


CORE = 1
ORDER = ((8, 4, 2), (4, 2, 8), (2, 8, 4))
PARTNERS = (1, 2, 4, 8)
HALVES = (512, 256, 128, 64)


def bit(stride):
    return (lax.axis_index("dp") // stride) % 2


def partner(stride):
    return {"dp": lax.axis_index("dp") + stride * (1 - 2 * bit(stride))}


def across(k):
    return {"dp": lax.axis_index("dp") + sum(stride * (1 - 2 * bit(stride)) for stride in PARTNERS if k & stride)}


def greet(devices):
    barrier = pltpu.get_barrier_semaphore()
    for device in devices:
        pl.semaphore_signal(barrier, inc=1, device_id=device, device_id_type=pl.DeviceIdType.MESH)
    pl.semaphore_wait(barrier, len(devices))


def some(start, n):
    return pl.ds(pl.multiple_of(start, 64), n)


def strides(c):
    return (CORE,) + ORDER[c]


class Scatter:
    def __init__(self, g, got, sent, send_sem, recv_sem):
        self.g, self.got, self.sent, self.send_sem, self.recv_sem = g, got, sent, send_sem, recv_sem

    def total(self, tile, c, keep):
        def read(ref, first):
            start = sum(b * HALVES[i] for i, b in enumerate(keep) if i >= first)
            return ref[tile % ref.shape[0], c, some(start, HALVES[len(keep) - 1]), :].astype(F32)
        out = read(self.g, 0)
        for stage in range(min(4, len(keep) if self.whole else len(keep) - 1)):
            out = out + read(self.got[stage], stage + 1)
        return out

    def copy(self, tile, c, stage):
        if stage == 0:
            src = self.g.at[tile % self.g.shape[0], c, some((1 - bit(CORE)) * 512, 512), :]
        else:
            src = self.sent[stage - 1].at[tile % self.sent[stage - 1].shape[0], c]
        got = self.got[stage]
        return pltpu.make_async_remote_copy(
            src_ref=src, dst_ref=got.at[tile % got.shape[0], c], send_sem=self.send_sem.at[stage, c, tile % 3], recv_sem=self.recv_sem.at[stage, c, tile % 3],
            device_id=partner(strides(c)[stage]), device_id_type=pl.DeviceIdType.MESH)

    def begin(self, tile):
        for c in range(3):
            self.copy(tile, c, 0).start()

    def advance(self, tile, stage):
        self.whole = False
        for c in range(3):
            self.copy(tile, c, stage - 1).wait_recv()
            if stage == 3:
                self.copy(tile, c, 1).wait_send()
            bits = [bit(s) for s in strides(c)]
            sent = self.sent[stage - 1]
            sent[tile % sent.shape[0], c] = self.total(tile, c, bits[:stage] + [1 - bits[stage]]).astype(BF)
            self.copy(tile, c, stage).start()

    def finish(self, tile, put, squares_ref):
        self.whole = True
        for c in range(3):
            self.copy(tile, c, 3).wait_recv()
            out = self.total(tile, c, [bit(s) for s in strides(c)]).astype(BF)
            put(c, out)
            squares = out.astype(F32) * out.astype(F32)
            squares_ref[...] += sum(squares[8 * i:8 * i + 8, 128 * j:128 * j + 128] for i in range(8) for j in range(FT // 128))
            for stage in (0, 2, 3):
                self.copy(tile, c, stage).wait_send()


class Gather:
    def __init__(self, full, hbm, own_sem, send_sem, recv_sem):
        self.full, self.hbm, self.own_sem, self.send_sem, self.recv_sem = full, hbm, own_sem, send_sem, recv_sem

    def place(self, tile, c, n):
        start = sum(bit(s) * HALVES[i] for i, s in enumerate(strides(c)) if HALVES[i] >= n)
        return self.full.at[tile, c, some(start, n), :]

    def put(self, tile):
        def store(c, out):
            self.place(tile, c, 64)[...] = out
        return store

    def copy(self, tile, c, stage):
        place = self.place(tile, c, 64 << stage)
        return pltpu.make_async_remote_copy(
            src_ref=place, dst_ref=place, send_sem=self.send_sem.at[tile, stage, c], recv_sem=self.recv_sem.at[tile, stage, c],
            device_id=partner(strides(c)[3 - stage]), device_id_type=pl.DeviceIdType.MESH)

    def store(self, tile):
        return pltpu.make_async_copy(self.full.at[tile], self.hbm.at[tile], self.own_sem.at[tile])

    def begin(self, tile):
        for c in range(3):
            self.copy(tile, c, 0).start()

    def advance(self, tile, stage):
        for c in range(3):
            self.copy(tile, c, stage - 1).wait_recv()
            self.copy(tile, c, stage).start()

    def finish(self, tile):
        for c in range(3):
            self.copy(tile, c, 3).wait_recv()
            for stage in range(4):
                self.copy(tile, c, stage).wait_send()
        self.store(tile).start()


def gather_scratch(tiles):
    return [pltpu.VMEM((tiles, 3, D, FT), BF), pltpu.SemaphoreType.DMA((tiles,)), pltpu.SemaphoreType.DMA((tiles, 4, 3)),
            pltpu.SemaphoreType.DMA((tiles, 4, 3))]


def scatter_scratch(slots, got_slots, sent_slots):
    return ([pltpu.VMEM((slots, 3, D, FT), BF)] + [pltpu.VMEM((k, 3, n, FT), BF) for k, n in zip(got_slots, HALVES, strict=True)]
            + [pltpu.VMEM((k, 3, n, FT), BF) for k, n in zip(sent_slots, HALVES[1:], strict=True)]
            + [pltpu.SemaphoreType.DMA((4, 3, 3)), pltpu.SemaphoreType.DMA((4, 3, 3))])


def scatter_of(refs):
    return Scatter(refs[0], refs[1:5], refs[5:8], refs[8], refs[9])


EARLY = 2


def kernel_b(h_hbm, dy_hbm, wg_ref, wu_ref, wd_ref, full_hbm, late_hbm, squares_ref, dh_hbm,
             a_ref, dy_ref, accg_ref, accu_ref, hid_ref, dg_ref, du_ref, sem, shard_ref, *rest):
    t = pl.program_id(0)
    s = scatter_of(rest[:10])
    g = Gather(rest[10], full_hbm, *rest[11:])
    store_late = pltpu.make_async_copy(shard_ref, late_hbm, sem.at[3])
    load_h = pltpu.make_async_copy(h_hbm, a_ref, sem.at[0])
    load_dy = pltpu.make_async_copy(dy_hbm, dy_ref, sem.at[1])
    store_dh = pltpu.make_async_copy(dy_ref, dh_hbm, sem.at[2])

    @pl.when(t == 0)
    def _():
        load_h.start()
        load_dy.start()
        greet([partner(stride) for stride in PARTNERS])
        squares_ref[...] = jnp.zeros_like(squares_ref)

        def clear(i, _):
            accg_ref[rows(i, 64), :] = jnp.zeros((64, D), F32)
            accu_ref[rows(i, 64), :] = jnp.zeros((64, D), F32)
            return 0
        lax.fori_loop(0, T // 64, clear, 0)
        load_h.wait()
        norm_into(a_ref, a_ref)
        load_dy.wait()

    def body(i):
        r = rows(i, MB)
        a = a_ref[r, :]
        gate = dot(a, wg_ref[0])
        up = dot(a, wu_ref[0])
        dhid = dot(dy_ref[r, :], wd_ref[0], NTR)
        hid, dg, du = back_elementwise(gate, up, dhid)
        hid_ref[r, :] = hid
        dg_ref[r, :] = dg
        du_ref[r, :] = du
        yg = dot(dg, wg_ref[0], NTR)
        yu = dot(du, wu_ref[0], NTR)
        accg_ref[r, :] += yg
        accu_ref[r, :] += yu

    def behind(steps, do, last=NT, first=0):
        @pl.when((t >= steps + first) & (t < steps + last) & (t < NT))
        def _():
            do(t - steps)

    def early(tile):
        s.finish(tile, g.put(tile), squares_ref)
        g.begin(tile)

    def late(tile):
        def put(c, out):
            shard_ref[tile - EARLY, c] = out
        s.finish(tile, put, squares_ref)

    def first_loop(i, _):
        body(i)

        @pl.when(i == 1)
        def _():
            behind(2, lambda tile: s.advance(tile, 3))
            behind(1, lambda tile: s.advance(tile, 1))
            behind(3, lambda tile: g.advance(tile, 2), EARLY)
        return 0

    def second_loop(n, _):
        weight_grads(a_ref, dy_ref, hid_ref, dg_ref, du_ref, s.g, t % 2, n)

        @pl.when(n == 0)
        def _():
            behind(1, lambda tile: s.advance(tile, 2))
            behind(3, lambda tile: g.advance(tile, 3), EARLY)
        return 0

    @pl.when(t < NT)
    def _():
        lax.fori_loop(0, T // MB, first_loop, 0)
        behind(2, early, EARLY)
        behind(2, late, NT, EARLY)
        behind(4, g.finish, EARLY)
        lax.fori_loop(0, D // 512, second_loop, 0)
        behind(0, s.begin)
        behind(2, lambda tile: g.advance(tile, 1), EARLY)

    @pl.when(t == NT)
    def _():
        load_h.start()
        s.advance(NT - 2, 3)
        s.advance(NT - 1, 1)
        load_h.wait()

        def fin(i, _):
            r = rows(i, 256)
            wide = a_ref[r, :].astype(F32)
            scale = lax.rsqrt(jnp.mean(wide * wide, -1, keepdims=True) + 1e-6)
            da = (accg_ref[r, :].astype(BF).astype(F32) + accu_ref[r, :].astype(BF).astype(F32)).astype(BF).astype(F32)
            inner = jnp.mean(da * wide, -1, keepdims=True)
            dn = (da * scale - wide * (scale * scale * scale * inner)).astype(BF).astype(F32)
            dh = (dy_ref[r, :].astype(F32) + dn).astype(BF)
            dy_ref[r, :] = dh
            return 0
        lax.fori_loop(0, T // 256, fin, 0)
        store_dh.start()
        s.advance(NT - 1, 2)
        late(NT - 2)
        g.finish(NT - 4)
        s.advance(NT - 1, 3)
        late(NT - 1)
        store_late.start()
        store_dh.wait()
        for tile in range(EARLY):
            g.store(tile).wait()
        store_late.wait()


def layer1(h1, dy, wg, wu, wd):
    any_ = pl.BlockSpec(memory_space=pl.ANY)
    at = lambda t: jnp.minimum(t, NT - 1)
    return pl.pallas_call(
        kernel_b,
        grid=(NT + 1,),
        in_specs=[any_, any_,
                  pl.BlockSpec((1, D, FT), lambda t: (1, 0, at(t))),
                  pl.BlockSpec((1, D, FT), lambda t: (1, 0, at(t))),
                  pl.BlockSpec((1, FT, D), lambda t: (1, at(t), 0))],
        out_specs=[any_, any_, pl.BlockSpec((8, 128), lambda t: (0, 0)), any_],
        out_shape=[jax.ShapeDtypeStruct((EARLY, 3, D, FT), BF), jax.ShapeDtypeStruct((NT - EARLY, 3, 64, FT), BF),
                   jax.ShapeDtypeStruct((8, 128), F32), jax.ShapeDtypeStruct((T, D), BF)],
        scratch_shapes=[pltpu.VMEM((T, D), BF), pltpu.VMEM((T, D), BF),
                        pltpu.VMEM((T, D), F32), pltpu.VMEM((T, D), F32),
                        pltpu.VMEM((T, FT), BF), pltpu.VMEM((T, FT), BF), pltpu.VMEM((T, FT), BF), pltpu.SemaphoreType.DMA((4,)),
                        pltpu.VMEM((NT - EARLY, 3, 64, FT), BF)]
        + scatter_scratch(2, (3, 3, 2, 2), (1, 2, 2)) + gather_scratch(EARLY),
        compiler_params=params(collective_id=1, has_side_effects=True),
        cost_estimate=pl.CostEstimate(flops=16 * T * D * F, bytes_accessed=12 * D * F + 6 * T * D, transcendentals=0),
        name="layer1",
    )(h1, dy, wg, wu, wd)


def kernel_c(a_hbm, dh_ref, gate_ref, up_ref, wd_ref, squares1_ref, shard_ref, factor_ref,
             a_ref, sem, hid_ref, dg_ref, du_ref, squares_ref, xs, xr, x_send, x_recv, *rest):
    t = pl.program_id(0)
    s = scatter_of(rest)
    load_a = pltpu.make_async_copy(a_hbm, a_ref, sem.at[0])

    def put(c, out):
        shard_ref[c] = out

    def behind(steps, do):
        @pl.when((t >= steps) & (t < steps + NT))
        def _():
            do(t - steps)

    @pl.when(t == 0)
    def _():
        load_a.start()
        greet([across(k) for k in range(1, 16)])
        squares_ref[...] = squares1_ref[...]

    @pl.when(t < NT)
    def _():
        def body(i, _):
            r = rows(i, MB)
            dhid = dot(dh_ref[r, :], wd_ref[0], NTR)
            hid, dg, du = back_elementwise(gate_ref[r, :], up_ref[r, :], dhid)
            hid_ref[r, :] = hid
            dg_ref[r, :] = dg
            du_ref[r, :] = du
            return 0
        lax.fori_loop(0, T // MB, body, 0)

    @pl.when(t == 0)
    def _():
        load_a.wait()

    behind(1, lambda tile: s.advance(tile, 1))
    def loop(n, _):
        @pl.when(t < NT)
        def _():
            weight_grads(a_ref, dh_ref, hid_ref, dg_ref, du_ref, s.g, t % 3, n)

        @pl.when(n == 0)
        def _():
            behind(2, lambda tile: s.advance(tile, 3))
        return 0
    lax.fori_loop(0, D // 512, loop, 0)
    behind(2, lambda tile: s.finish(tile, put, squares_ref))
    behind(0, s.begin)
    behind(1, lambda tile: s.advance(tile, 2))

    @pl.when(t == NT + 1)
    def _():
        xs[...] = squares_ref[...]
        copies = [pltpu.make_async_remote_copy(src_ref=xs, dst_ref=xr.at[k], send_sem=x_send.at[k], recv_sem=x_recv.at[k],
                                               device_id=across(k), device_id_type=pl.DeviceIdType.MESH) for k in range(1, 16)]
        for copy in copies:
            copy.start()
        for copy in copies:
            copy.wait()
        terms = [squares_ref[...]] + [xr[k] for k in range(1, 16)]
        while len(terms) > 1:
            terms = [one + two for one, two in zip(terms[::2], terms[1::2], strict=True)]
        total = terms[0]
        total = jnp.sum(jnp.sum(total, 0, keepdims=True), 1, keepdims=True)
        factor_ref[...] = jnp.broadcast_to(jnp.minimum(1.0, 0.5 * lax.rsqrt(total / (6 * D * F) + 1e-30)), (8, 128))


def back0(a0, dh1, gate, up, wd, squares1):
    whole = pl.BlockSpec((T, D), lambda t: (0, 0), pipeline_mode=pl.Buffered(1))
    any_ = pl.BlockSpec(memory_space=pl.ANY)
    at = lambda t: jnp.minimum(t, NT - 1)
    return pl.pallas_call(
        kernel_c,
        grid=(NT + 2,),
        in_specs=[any_, whole, pl.BlockSpec((T, FT), lambda t: (0, at(t))), pl.BlockSpec((T, FT), lambda t: (0, at(t))),
                  pl.BlockSpec((1, FT, D), lambda t: (0, at(t), 0)),
                  pl.BlockSpec((8, 128), lambda t: (0, 0))],
        out_specs=[pl.BlockSpec((3, 64, FT), lambda t: (0, 0, jnp.maximum(t - 2, 0))),
                   pl.BlockSpec((8, 128), lambda t: (0, 0))],
        out_shape=[jax.ShapeDtypeStruct((3, 64, F), BF), jax.ShapeDtypeStruct((8, 128), F32)],
        scratch_shapes=[pltpu.VMEM((T, D), BF), pltpu.SemaphoreType.DMA((1,)),
                        pltpu.VMEM((T, FT), BF), pltpu.VMEM((T, FT), BF), pltpu.VMEM((T, FT), BF), pltpu.VMEM((8, 128), F32),
                        pltpu.VMEM((8, 128), F32), pltpu.VMEM((16, 8, 128), F32), pltpu.SemaphoreType.DMA((16,)), pltpu.SemaphoreType.DMA((16,))]
        + scatter_scratch(3, (3, 3, 3, 3), (3, 3, 3)),
        compiler_params=params(collective_id=2, has_side_effects=True),
        cost_estimate=pl.CostEstimate(flops=8 * T * D * F, bytes_accessed=8 * T * F + 8 * D * F, transcendentals=0),
        name="back0",
    )(a0, dh1, gate, up, wd, squares1)


FB = 256


def adamw(w, m, v, g):
    m = 0.9 * m + 0.1 * g
    v = 0.95 * v + 0.05 * g * g
    w = w.astype(F32)
    return (w - 0.02 * (m * lax.rsqrt(v + 1e-8) + 0.1 * w)).astype(BF), m, v


def update(refs, outs, i, where, g):
    at = (0,) + where
    new = adamw(refs[i][at], refs[3 + i][at], refs[6 + i][at], g)
    for k in range(3):
        outs[3 * k + i][at] = new[k]


def owner(c, k):
    return sum(s * (k * 64 // HALVES[i] % 2) for i, s in enumerate(strides(c)))


def update_all(refs, outs, factor, gathered):
    for k in range(8):
        both = slice(128 * k, 128 * k + 128)
        for i in range(3):
            g = jnp.concatenate([gathered(owner(i, 2 * k + half), i) for half in range(2)], 0).astype(F32)
            where = (slice(None), both) if i == 2 else (both, slice(None))
            update(refs, outs, i, where, (g.T if i == 2 else g) * factor)


def kernel_o1(f_ref, early_ref, late_ref, *refs):
    ins, outs = refs[:9], refs[-9:]
    factor = f_ref[0:1, 0:1]
    early = EARLY * FT // FB

    @pl.when(pl.program_id(0) < early)
    def _():
        for i in range(3):
            g = early_ref[0, i].astype(F32)
            update(ins, outs, i, (slice(None), slice(None)), (g.T if i == 2 else g) * factor)

    @pl.when(pl.program_id(0) >= early)
    def _():
        update_all(ins, outs, factor, lambda device, i: late_ref[device, 0, i])


def kernel_o0(f_ref, g_ref, *refs):
    update_all(refs[:9], refs[-9:], f_ref[0:1, 0:1], lambda device, i: g_ref[device, i])


def optimizer(layer, kernel, factor, gradients, specs, arrays, before):
    wide = pl.BlockSpec((1, D, FB), lambda t: (layer, 0, t))
    tall = pl.BlockSpec((1, FB, D), lambda t: (layer, t, 0))
    three = [wide, wide, tall]
    first = 1 + len(gradients) + 9
    return pl.pallas_call(
        kernel,
        grid=(F // FB,),
        in_specs=[pl.BlockSpec((8, 128), lambda t: (0, 0))] + specs + three * 3 + [pl.BlockSpec(memory_space=pl.ANY)] * len(before),
        out_specs=three * 3,
        out_shape=[jax.ShapeDtypeStruct(a.shape, a.dtype) for a in arrays],
        input_output_aliases={first + i: i for i in range(len(before))},
        compiler_params=params(),
        cost_estimate=pl.CostEstimate(flops=30 * D * F, bytes_accessed=66 * D * F, transcendentals=3 * D * F),
        name=f"adamw{layer}",
    )(factor, *gradients, *arrays, *before)


def solution(mesh):
    def step(x, dy, *arrays):
        wg, wu, wd = arrays[:3]
        gate, up, h1, a0 = forward0(x[0], wg, wu, wd)
        early, late, squares1, dh1 = layer1(h1, dy[0], wg, wu, wd)
        late = lax.all_gather(late, "dp")
        s0, factor = back0(a0, dh1, gate, up, wd, squares1)
        full0 = lax.all_gather(s0, "dp")
        n, blocks = EARLY * FT // FB, FT // FB
        specs = [pl.BlockSpec((1, 3, D, FB), lambda t: (jnp.minimum(t, n - 1) // blocks, 0, 0, jnp.minimum(t, n - 1) % blocks)),
                 pl.BlockSpec((16, 1, 3, 64, FB), lambda t: (0, jnp.maximum(t - n, 0) // blocks, 0, 0, jnp.maximum(t - n, 0) % blocks))]
        new = optimizer(1, kernel_o1, factor, (early, late), specs, arrays, ())
        specs = [pl.BlockSpec((16, 3, 64, FB), lambda t: (0, 0, 0, t))]
        return tuple(optimizer(0, kernel_o0, factor, (full0,), specs, arrays, new))

    return jax.shard_map(
        step,
        mesh=mesh,
        in_specs=(P(("rep", "dp"), None, None),) * 2 + (P(None, None, None),) * 9,
        out_specs=(P("rep", None, None),) * 9,
        check_vma=False,
    )
```

time: 446 us -> 440 us (0.987)
  Pallas kernels: 427 us -> 417 us
    pallas_call x1, Pallas kernels: 145 us -> 139 us  [layer1(): pl.pallas_call(kernel_b, grid=(NT + 1,), in_specs=[any_, any_, pl.BlockSp...]
  transfers between devices with their start and end apart: 1 -> 2, of which waited for: 1 -> 1; matrix products, arithmetic and copies ran while one was open for 0% -> 0% of each run, Pallas kernels for 15% -> 40%
where the time goes in v3:
time: 440 us
  Pallas kernels  417 us (95%)
  between operations  14.1 us (3%)
  waiting for transfers between devices  8.68 us (2%)
    pallas_call x1, Pallas kernels, layer1(): pl.pallas_call(kernel_b, grid=(NT + 1,), in_specs=[any_, any_, pl.BlockSp...  139 us
    pallas_call x2, Pallas kernels, optimizer(): pl.pallas_call(kernel, grid=(F // FB,), in_specs=[pl.BlockSpec((8, 128),...  121 us
    pallas_call x1, Pallas kernels, back0(): pl.pallas_call(kernel_c, grid=(NT + 2,), in_specs=[any_, whole, pl.BlockS...  110 us
    pallas_call x1, Pallas kernels, forward0(): pl.pallas_call(kernel_a, grid=(NT,), in_specs=[whole, pl.BlockSpec((1, D,...  46.8 us
  transfers between devices with their start and end apart: 2, of which 1 were waited for; matrix products, arithmetic and copies ran while one was open for 0% of the time, Pallas kernels for 40%

profile of v3, /device:TPU:0, one launch (start us, length us, event | category | flops | bytes accessed | tf_op | source)
XLA Modules:
  0.0 440.1 jit_solution(7966356522033404608)
XLA Ops:
  7.2 0.0 all-gather.7.cloned.1.call-start
  7.2 46.8 %fwd0.1 = (f32[2048,2560]{1,0:T(8,128)}, f32[2048,2560]{1,0:T(8,128)}, bf16[2048,1024]{1,0:T(8,128)(2,1)}, bf16[2048,1024]{1,0:T(8,128)(2,1)}) custom-call(bf16[2048,1024]{1,0:T(8,128)(2,1)} %bitcast.6, bf16[2,1024,2560]{2,1,0:T(8,128)(2,1)} %refs_0_.3, bf16[2,1024,2560]{2,1,0:T(8,128)(2,1)} %refs_1_.3, bf16[2,2560,1024]{2,1,0:T(8,128)(2,1)} %refs_2_.3), custom_call_target="tpu_custom_call" | custom-call | flops 32212254720 | bytes 57671680 | tf_op jit(solution)/shard_map/fwd0/pallas_call | solution.py:86
  54.0 138.9 %layer1.1 = (bf16[2,3,1024,512]{3,2,1,0:T(8,128)(2,1)}, bf16[3,3,64,512]{3,2,1,0:T(8,128)(2,1)}, f32[8,128]{1,0:T(8,128)}, bf16[2048,1024]{1,0:T(8,128)(2,1)}) custom-call(bf16[2048,1024]{1,0:T(8,128)(2,1)} %get-tuple-element.29.h_hbm, bf16[2048,1024]{1,0:T(8,128)(2,1)} %bitcast.7, bf16[2,1024,2560]{2,1,0:T(8,128)(2,1)} %refs_0_.3, ...), custom_call_target="tpu_custom_call" | custom-call | flops 85899345920 | bytes 44040192 | tf_op jit(solution)/shard_map/layer1/pallas_call | solution.py:378
  192.9 0.0 all-gather.7.cloned.1.call-update
  192.9 0.0 all-gather.5.cloned.1.call-start
  193.0 110.0 %back0.1 = (bf16[3,64,2560]{2,1,0:T(8,128)(2,1)}, f32[8,128]{1,0:T(8,128)}) custom-call(bf16[2048,1024]{1,0:T(8,128)(2,1)} %get-tuple-element.28.a_hbm, bf16[2048,1024]{1,0:T(8,128)(2,1)} %get-tuple-element.30.dh_ref, f32[2048,2560]{1,0:T(8,128)} %get-tuple-element.31.gate_ref, f32[2048,2560]{1,0:T(8,128)} %get-tuple-element.32.up_ref, ...), custom_call_target="tpu_custom_call" | custom-call | flops 42949672960 | bytes 62914560 | tf_op jit(solution)/shard_map/back0/pallas_call | solution.py:471
  303.0 0.0 all-gather.5.cloned.1.call-update
  303.1 0.0 all-gather.7.cloned.1.call-done
  303.1 64.0 %adamw1.1 = (bf16[2,1024,2560]{2,1,0:T(8,128)(2,1)}, bf16[2,1024,2560]{2,1,0:T(8,128)(2,1)}, bf16[2,2560,1024]{2,1,0:T(8,128)(2,1)}, f32[2,1024,2560]{2,1,0:T(8,...) custom-call(f32[8,128]{1,0:T(8,128)} %get-tuple-element.34.f_ref, ...), custom_call_target="tpu_custom_call" | custom-call | flops 78643200 | bytes 173015040 | tf_op jit(solution)/shard_map/adamw1/pallas_call | solution.py:545
  367.1 8.6 %all-gather.5.cloned.1.call-done = bf16[48,64,2560]{2,1,0:T(8,128)(2,1)} async-done(((bf16[3,64,2560]{2,1,0:T(8,128)(2,1)}), bf16[48,64,2560]{2,1,0:T(8,128)(2,1)}) %all-gather.5.cloned.1.call-update) | async-done | bytes 15728656 | tf_op jit(solution)/shard_map/all_gather | solution.py:565
  375.8 57.5 %adamw0.1 = (bf16[2,1024,2560]{2,1,0:T(8,128)(2,1)}, bf16[2,1024,2560]{2,1,0:T(8,128)(2,1)}, bf16[2,2560,1024]{2,1,0:T(8,128)(2,1)}, f32[2,1024,2560]{2,1,0:T(8,...) custom-call(f32[8,128]{1,0:T(8,128)} %get-tuple-element.34.f_ref, ...), custom_call_target="tpu_custom_call", output_to_operand_aliasing={{0}: (11, {}), {1}: (12, {}), {2}: (13, {}), {3}: (14, {}),... | custom-call | flops 78643200 | bytes 173015040 | tf_op jit(solution)/shard_map/adamw0/pallas_call | solution.py:545
Async XLA Ops:
  7.2 295.9 %all-gather.7.cloned.1.call-start = ((), (), s32[]{:S(2)}) async-start(), calls=%async_computation.1 | async-start | bytes 10027008 | tf_op jit(solution)/shard_map/all_gather | solution.py:563
  192.9 182.8 %all-gather.5.cloned.1.call-start = ((), (), s32[]{:S(2)}) async-start(), calls=%async_computation | async-start | bytes 16711680 | tf_op jit(solution)/shard_map/all_gather | solution.py:565
Sparse Core Ops, SparseCore 0:
  193.1 65.4 all-gather.6
  303.2 72.5 all-gather.4
